TPU v7x, 256 devices: a whole 4x4x8 slice. The times are simulated.
256 devices in a mesh: slab: 128 (over z, y, x), feat: 2 (over core).
Axes of the slice: x: 4, y: 4, z: 8, core: 2. Of those that a mesh axis runs over, the one named last changes fastest.
Arguments:
- states: float32 [40, 65536], P(None, ('slab', 'feat')), may hold values from -6 to 6
- inputs: float32 [65536], P(('slab', 'feat')), may hold values from -4 to 4
- targets: float32 [40, 65536], P(None, ('slab', 'feat')), may hold values from -4 to 4
Outputs:
- local_operators: float32 [128, 40, 862], P('slab', 'feat')
- scaled_duals: float32 [128, 40, 862], P('slab', 'feat')
- consensus: float32 [40, 862], P('feat')
- residual_history: float32 [2, 2], replicated
All inputs are finite; a program needn't handle non-finite values.
Results may differ from a plain program's by a relative error of at most 0.0003.
Values sent between devices are 32-bit elements; how exact they have to be, the bound alone decides.
A program may use at most 64 MiB of HBM per device.

v0:
```python
import jax
import jax.numpy as jnp
from jax import lax
from jax.sharding import Mesh
from jax.sharding import PartitionSpec as P

ITERS = 2
SLAB = ("slab_0", "slab_1", "slab_2")
SLAB_FEAT = ("slab_0", "slab_1", "slab_2", "feat")


penalty = 1.0


def total_of_pieces(array, axis):
    tiles = lax.all_gather(array, axis)
    return tiles.sum(axis=0)


def rows_first(arrays, axis, dims):
    turned = [jnp.moveaxis(a, dim, 0) for a, dim in zip(arrays, dims)]
    widths = [t[0].size for t in turned]
    both = jnp.concatenate([t.reshape(-1, w) for t, w in zip(turned, widths)], axis=1)
    whole = lax.all_gather(both, axis, axis=0, tiled=True)
    tiles = jnp.split(whole, [sum(widths[:k]) for k in range(1, len(widths))], axis=1)
    return tuple(
        (
            jnp.moveaxis(b.reshape(-1, *t.shape[1:]), 0, dim)
            for b, t, dim in zip(tiles, turned, dims)
        )
    )


def by_axis(array, axes):
    for axis in axes:
        array = lax.psum(array, axis)
    return array


def features(states, inputs):
    reduced = states.shape[0]
    blocks = [states]
    for column in range(reduced):
        blocks.append(states[column : column + 1] * states[column:])
    blocks.append(inputs[None, :])
    blocks.append(jnp.ones_like(inputs)[None, :])
    return jnp.concatenate(blocks, 0)


def product(left, right):
    return jnp.dot(left, right, precision=lax.Precision.HIGHEST, preferred_element_type=jnp.float32)


def solve_rows(factor, right_side):
    return jax.scipy.linalg.cho_solve((factor, True), right_side.T).T


def slab_average(summand):
    return total_of_pieces(summand, SLAB)


def shards(states, inputs, targets):
    reduced = states.shape[0]
    feat_count = lax.axis_size("feat")
    slab_count = lax.axis_size(SLAB)
    half_rows = reduced // feat_count
    all_states, all_targets, all_inputs = rows_first((states, targets, inputs), "feat", (1, 1, 0))
    design = features(all_states, all_inputs)
    row_total = design.shape[1]
    gram_matrix = product(design, design.T) / row_total
    first_row = lax.axis_index("feat") * half_rows
    picked = lax.dynamic_slice_in_dim(all_targets, first_row, half_rows, 0)
    cross = product(picked, design.T) / row_total
    width = gram_matrix.shape[0]
    factor = jnp.linalg.cholesky(gram_matrix + penalty * jnp.eye(width, dtype=jnp.float32))
    consensus = jnp.zeros((half_rows, width), jnp.float32)
    duals = jnp.zeros((half_rows, width), jnp.float32)
    operator_rows = duals
    primal_list = []
    dual_list = []
    for sweep in range(ITERS):
        operator_rows = solve_rows(factor, cross + penalty * (consensus - duals))
        updated = slab_average(operator_rows + duals) / slab_count
        duals = duals + operator_rows - updated
        primal_part = jnp.sum(jnp.square(operator_rows - updated))
        dual_part = penalty * penalty * jnp.sum(jnp.square(updated - consensus))
        primal_sum, dual_sum = (by_axis(primal_part, SLAB_FEAT), by_axis(dual_part, SLAB_FEAT))
        primal_list.append(primal_sum)
        dual_list.append(dual_sum)
        consensus = updated
    history = jnp.stack([jnp.stack(primal_list), jnp.stack(dual_list)])
    residual_history = jnp.sqrt(history / (slab_count * reduced * width))
    return (operator_rows[None], duals[None], consensus, residual_history)


def solution(mesh):
    split = Mesh(
        mesh.devices.reshape(8, 4, 4, mesh.shape["feat"]), ("slab_0", "slab_1", "slab_2", "feat")
    )
    return jax.shard_map(
        shards,
        mesh=split,
        in_specs=(P(None, SLAB_FEAT), P(SLAB_FEAT), P(None, SLAB_FEAT)),
        out_specs=(P(SLAB, "feat", None), P(SLAB, "feat", None), P("feat", None), P()),
        check_vma=False,
    )
```

profile of v0, /device:TPU:1, one launch (start us, length us, event | category | flops | bytes accessed | tf_op | source)
XLA Modules:
  0.0 660.4 jit_solution(3695795320718135102)
XLA Ops:
  8.6 4.8 all_gather.15
  24.2 13.3 %concatenate.49 = f32[862,512]{1,0:T(8,128)S(1)} concatenate(f32[40,512]{1,0:T(8,128)S(1)} %get-tuple-element.61, f32[40,512]{1,0:T(8,128)S(1)} %broadcast_multiply_fusion.1, f32[39,512]{1,0:T(8,128)S(1)} %slice_multiply_fusion.6, f32[38,512]{1,0:T(8,128)S(1)} %slice_multiply_fusion.5, f32[37,512]{1,0:T(8,128)S(1)} %slice_multiply_fusion.4, f32[36,512]{1,0:T(8,128)S(1)} %slice_multiply_fusion.3, ...), dimensions={0} | concatenate | bytes 3530752 | tf_op jit(solution)/shard_map/concatenate | solution.py:47
  37.5 7.8 %convert_add_fusion = (f32[862,862]{0,1:T(8,128)}, f32[862,862]{0,1:T(8,128)}) fusion(f32[862,512]{1,0:T(8,128)S(1)} %concatenate.49), kind=kOutput, calls=%fused_computation.8 | convolution fusion | flops 4568234496 | bytes 7709728 | tf_op jit(solution)/shard_map/dot_general | solution.py:51
  45.4 3.6 copy.12
  49.0 2.3 fusion.1
  51.3 1.6 copy-done.3
  52.9 11.7 %cholesky.196 = f32[128,128]{1,0:T(8,128)S(1)} custom-call(f32[128,128]{1,0:T(8,128)S(1)} %cholesky.508), custom_call_target="Cholesky" | custom-call | tf_op jit(solution)/shard_map/jit(cholesky)/cholesky | solution.py:75
  64.7 9.8 %custom-call.56 = f32[1,128,128]{1,2,0:T(8,128)S(1)} custom-call(f32[1,128,128]{2,1,0:T(8,128)S(1)} %get-tuple-element.118), custom_call_target="InvertDiagBlocksLowerTriangular" | custom-call | tf_op jit(solution)/shard_map/jit(cholesky)/cholesky | solution.py:75
  74.7 1.4 constant_dynamic-update-slice_fusion.62
  76.1 1.5 convolution_subtract_fusion
  78.2 13.2 %cholesky.217 = f32[128,128]{1,0:T(8,128)} custom-call(f32[128,128]{1,0:T(8,128)} %cholesky.512), custom_call_target="Cholesky" | custom-call | tf_op jit(solution)/shard_map/jit(cholesky)/cholesky | solution.py:75
  91.4 1.5 select_reduce_fusion.4
  92.9 11.7 %custom-call.57 = f32[1,128,128]{1,2,0:T(8,128)} custom-call(f32[1,128,128]{2,1,0:T(8,128)} %get-tuple-element.115), custom_call_target="InvertDiagBlocksLowerTriangular" | custom-call | tf_op jit(solution)/shard_map/jit(cholesky)/cholesky | solution.py:75
  104.6 1.2 convolution_dynamic-update-slice_fusion
  105.8 1.6 convolution_subtract_fusion.1
  107.4 12.3 %cholesky.413 = f32[128,128]{1,0:T(8,128)} custom-call(f32[128,128]{1,0:T(8,128)S(1)} %cholesky.517), custom_call_target="Cholesky" | custom-call | tf_op jit(solution)/shard_map/jit(cholesky)/cholesky | solution.py:75
  121.4 10.4 %custom-call.58 = f32[1,128,128]{1,2,0:T(8,128)} custom-call(f32[1,128,128]{2,1,0:T(8,128)S(1)} %get-tuple-element.112), custom_call_target="InvertDiagBlocksLowerTriangular" | custom-call | tf_op jit(solution)/shard_map/jit(cholesky)/cholesky | solution.py:75
  133.0 1.7 convolution_subtract_fusion.2
  134.7 11.9 %cholesky.432 = f32[128,128]{1,0:T(8,128)S(1)} custom-call(f32[128,128]{1,0:T(8,128)S(1)} %cholesky.522), custom_call_target="Cholesky" | custom-call | tf_op jit(solution)/shard_map/jit(cholesky)/cholesky | solution.py:75
  147.3 9.8 %custom-call.59 = f32[1,128,128]{1,2,0:T(8,128)S(1)} custom-call(f32[1,128,128]{2,1,0:T(8,128)S(1)} %get-tuple-element.109), custom_call_target="InvertDiagBlocksLowerTriangular" | custom-call | tf_op jit(solution)/shard_map/jit(cholesky)/cholesky | solution.py:75
  157.4 1.7 convolution_subtract_fusion.3
  159.1 11.7 %cholesky.451 = f32[128,128]{1,0:T(8,128)S(1)} custom-call(f32[128,128]{1,0:T(8,128)S(1)} %cholesky.527), custom_call_target="Cholesky" | custom-call | tf_op jit(solution)/shard_map/jit(cholesky)/cholesky | solution.py:75
  171.6 9.8 %custom-call.60 = f32[1,128,128]{1,2,0:T(8,128)S(1)} custom-call(f32[1,128,128]{2,1,0:T(8,128)S(1)} %get-tuple-element.106), custom_call_target="InvertDiagBlocksLowerTriangular" | custom-call | tf_op jit(solution)/shard_map/jit(cholesky)/cholesky | solution.py:75
  181.7 1.5 convolution_subtract_fusion.4
  183.2 11.9 %cholesky.471 = f32[128,128]{1,0:T(8,128)S(1)} custom-call(f32[128,128]{1,0:T(8,128)S(1)} %cholesky.532), custom_call_target="Cholesky" | custom-call | tf_op jit(solution)/shard_map/jit(cholesky)/cholesky | solution.py:75
  195.8 9.8 %custom-call.61 = f32[1,128,128]{1,2,0:T(8,128)S(1)} custom-call(f32[1,128,128]{2,1,0:T(8,128)S(1)} %get-tuple-element.103), custom_call_target="InvertDiagBlocksLowerTriangular" | custom-call | tf_op jit(solution)/shard_map/jit(cholesky)/cholesky | solution.py:75
  207.0 8.6 %cholesky.492 = f32[94,94]{1,0:T(8,128)S(1)} custom-call(f32[94,94]{1,0:T(8,128)S(1)} %convolution_subtract_fusion.5), custom_call_target="Cholesky" | custom-call | tf_op jit(solution)/shard_map/jit(cholesky)/cholesky | solution.py:75
  223.3 18.0 %while.4 = (s32[]{:T(128)}, f32[862,862]{1,0:T(8,128)}, s32[6,2]{0,1:T(2,128)S(1)}, f32[6,128,128]{2,1,0:T(8,128)S(1)}, s32[]{:T(128)}) while((s32[]{:T(128)}, f32[862,862]{1,0:T(8,128)}, s32[6,2]{0,1:T(2,128)S(1)}, f32[6,128,128]{2,1,0:T(8,128)S(1)}, s32[]{:T(128)}) %tuple.121), condition=%wide.while_cond.clone, body=%wide.while_body.clone.sunk | while | flops 2 | bytes 131189 | solution.py:55
  224.0 2.3 bitcast_dynamic-update-slice_fusion.2
  227.0 2.3 bitcast_dynamic-update-slice_fusion.2
  230.0 2.3 bitcast_dynamic-update-slice_fusion.2
  233.0 2.3 bitcast_dynamic-update-slice_fusion.2
  236.0 2.3 bitcast_dynamic-update-slice_fusion.2
  239.0 2.3 bitcast_dynamic-update-slice_fusion.2
  243.2 69.8 %custom-call.64 = f32[7,128,128]{1,2,0:T(8,128)S(1)} custom-call(f32[7,128,128]{2,1,0:T(8,128)} %pad_maximum_fusion), custom_call_target="InvertDiagBlocksLowerTriangular" | custom-call | tf_op jit(solution)/shard_map/jit(_cho_solve)/triangular_solve | solution.py:55
  313.1 3.1 convolution_multiply_fusion
  327.0 131.4 %all-gather.7.cloned.1.call-done = f32[128,20,862]{2,1,0:T(8,128)} async-done(((f32[1,20,862]{2,1,0:T(8,128)}), f32[128,20,862]{2,1,0:T(8,128)}) %all-gather.7.cloned.1.call-update) | async-done | bytes 8826896 | tf_op jit(solution)/shard_map/all_gather | solution.py:16
  458.4 5.4 reduce_sum.54
  471.4 1.5 fusion.108
  473.7 127.5 %all-gather.9.cloned.1.call-done = f32[128,20,862]{2,1,0:T(8,128)} async-done(((f32[1,20,862]{2,1,0:T(8,128)}), f32[128,20,862]{2,1,0:T(8,128)}) %all-gather.9.cloned.1.call-update) | async-done | bytes 8826896 | tf_op jit(solution)/shard_map/all_gather | solution.py:16
  601.2 4.8 reduce_sum.55
  606.0 1.6 multiply_reduce_fusion.2
  609.2 12.5 %all-reduce.3 = (f32[]{:T(128)}, f32[]{:T(128)}, f32[]{:T(128)}, f32[]{:T(128)}) all-reduce(f32[]{:T(128)} %get-tuple-element.31, f32[]{:T(128)} %get-tuple-element.30, f32[]{:T(128)} %get-tuple-element.32, f32[]{:T(128)} %get-tuple-element.29), channel_id=1, replica_groups=mesh['slab_0'=8,'slab_1'=4,'slab_2'=4,'feat'=2] {'slab_0'}, use_global_device_ids=true, to_apply=%region_32.34 | all-reduce | flops 4 | bytes 32 | tf_op jit(solution)/shard_map/psum | solution.py:36
  621.7 9.1 %all-reduce.5 = (f32[]{:T(128)}, f32[]{:T(128)}, f32[]{:T(128)}, f32[]{:T(128)}) all-reduce(f32[]{:T(128)} %get-tuple-element.41, f32[]{:T(128)} %get-tuple-element.42, f32[]{:T(128)} %get-tuple-element.43, f32[]{:T(128)} %get-tuple-element.44), channel_id=1, replica_groups=mesh['slab_0'=8,'slab_1'=4,'slab_2'=4,'feat'=2] {'slab_1'}, use_global_device_ids=true, to_apply=%region_33.35 | all-reduce | flops 4 | bytes 32 | tf_op jit(solution)/shard_map/psum | solution.py:36
  630.8 7.2 %all-reduce.4 = (f32[]{:T(128)}, f32[]{:T(128)}, f32[]{:T(128)}, f32[]{:T(128)}) all-reduce(f32[]{:T(128)} %get-tuple-element.49, f32[]{:T(128)} %get-tuple-element.50, f32[]{:T(128)} %get-tuple-element.51, f32[]{:T(128)} %get-tuple-element.52), channel_id=1, replica_groups=mesh['slab_0'=8,'slab_1'=4,'slab_2'=4,'feat'=2] {'slab_2'}, use_global_device_ids=true, to_apply=%region_34.36 | all-reduce | flops 4 | bytes 32 | tf_op jit(solution)/shard_map/psum | solution.py:36
  638.0 11.9 %all-reduce.6 = (f32[1]{0:T(128)}, f32[1]{0:T(128)}, f32[1]{0:T(128)}, f32[1]{0:T(128)}) all-reduce(f32[1]{0:T(128)} %bitcast.84, f32[1]{0:T(128)} %bitcast.83, f32[1]{0:T(128)} %bitcast.81, f32[1]{0:T(128)} %bitcast.80), channel_id=1, replica_groups=mesh['slab_0'=8,'slab_1'=4,'slab_2'=4,'feat'=2] {'feat'}, use_global_device_ids=true, to_apply=%region_35.37 | all-reduce | flops 4 | bytes 32 | tf_op jit(solution)/shard_map/psum | solution.py:36
  649.9 1.3 maximum_bitcast_fusion.1
  651.2 1.3 maximum_bitcast_fusion
  (201 shorter events, 49.8 us)
Async XLA Ops:
  7.2 451.2 %all-gather.7.cloned.1.call-start = ((), (), s32[]{:S(2)}) async-start(), calls=%async_computation | async-start | bytes 11096064 | tf_op jit(solution)/shard_map/all_gather | solution.py:16
  37.5 7.8 %copy-start = (f32[862,512]{1,0:T(8,128)}, f32[862,512]{1,0:T(8,128)S(1)}, u32[]{:S(2)}) copy-start(f32[862,512]{1,0:T(8,128)S(1)} %concatenate.49) | copy-start | bytes 5296132
  51.3 1.6 copy-start.3
  221.4 0.9 copy-start.9
  221.4 1.9 copy-start.7
  221.7 1.7 copy-start.1
  241.4 75.0 %copy-start.2 = (f32[862,862]{1,0:T(8,128)S(1)}, f32[862,862]{1,0:T(8,128)}, u32[]{:S(2)}) copy-start(f32[862,862]{1,0:T(8,128)} %get-tuple-element.215) | copy-start | bytes 8916532
  316.1 10.8 %copy-start.6 = (f32[862,20]{0,1:T(8,128)}, f32[862,20]{0,1:T(8,128)S(1)}, u32[]{:S(2)}) copy-start(f32[862,20]{0,1:T(8,128)S(1)} %convolution_multiply_fusion) | copy-start | bytes 206884
  327.0 274.3 %all-gather.9.cloned.1.call-start = ((), (), s32[]{:S(2)}) async-start(), calls=%async_computation.1 | async-start | bytes 11096064 | tf_op jit(solution)/shard_map/all_gather | solution.py:16
  463.7 7.6 %copy-start.4 = (f32[20,862]{1,0:T(8,128)S(1)}, f32[20,862]{1,0:T(8,128)}, u32[]{:S(2)}) copy-start(f32[20,862]{1,0:T(8,128)} %reduce_sum.54) | copy-start | bytes 206884
  473.7 132.3 %copy-start.5 = (f32[20,862]{1,0:T(8,128)S(1)}, f32[20,862]{1,0:T(8,128)}, u32[]{:S(2)}) copy-start(f32[20,862]{1,0:T(8,128)} %reduce_sum.54) | copy-start | bytes 206884
  607.6 45.6 %copy-start.8 = (f32[20,862]{1,0:T(8,128)}, f32[20,862]{1,0:T(8,128)S(1)}, u32[]{:S(2)}) copy-start(f32[20,862]{1,0:T(8,128)S(1)} %get-tuple-element.57) | copy-start | bytes 206884
Sparse Core Ops, SparseCore 0:
  327.1 131.2 all-gather.6
  473.1 128.0 all-gather.8
where the time goes:
time: 667 us; the launch traced here: 660 us
  waiting for transfers between devices  259 us (39%)
  other arithmetic  252 us (38%)
  local copies, waits for them, and re-layouts  46.1 us (7%)
  blocking collectives  45.4 us (7%)
  matrix products  37.7 us (6%)
  between operations  20 us (3%)
    all_gather x2, waiting for transfers between devices, total_of_pieces(): tiles = lax.all_gather(array, axis)  259 us
    another operation x26, other arithmetic, shards(): jnp.linalg.cholesky(gram_matrix + penalty * jnp.eye(width, dtype=jnp.floa...  149 us
    another operation x8, other arithmetic, solve_rows(): return jax.scipy.linalg.cho_solve((factor, True), right_side.T).T  72.5 us
    psum x4, blocking collectives, by_axis(): array = lax.psum(array, axis)  40.7 us
    another operation x26, local copies, waits for them, and re-layouts, solve_rows(): return jax.scipy.linalg.cho_solve((factor, True), right_side.T).T  19.2 us
    another operation x12, matrix products, shards(): jnp.linalg.cholesky(gram_matrix + penalty * jnp.eye(width, dtype=jnp.floa...  13.7 us
  transfers between devices with their start and end apart: 2, of which 2 were waited for; matrix products, arithmetic and copies ran while one was open for 0% of the time, Pallas kernels for 0%

commit v1 on v0

v1 whole, which is shorter than its diff:
```python
import functools

import jax
import jax.numpy as jnp
from jax import lax
from jax.experimental import pallas as pl
from jax.experimental.pallas import tpu as pltpu
from jax.sharding import PartitionSpec as P

F32, BF16 = jnp.float32, jnp.bfloat16
NN = (((1,), (0,)), ((), ()))
NT = (((1,), (1,)), ((), ()))
TN = (((0,), (0,)), ((), ()))
MESH = pl.DeviceIdType.MESH

R = 40
HALF = 20
FEATS = 862
WIDE = 896
PLANE = 16
DEPTH = 8
N_SLAB = 128
M = 512
MINE = 256
rho = 1.0


def dot(a, b, dims):
    return lax.dot_general(a, b, dims, preferred_element_type=F32)


def two(a):
    high = a.astype(BF16)
    return high, (a - high.astype(F32)).astype(BF16)


def dot3(a, b, dims):
    (ah, al), (bh, bl) = a, b
    return dot(ah, bh, dims) + (dot(ah, bl, dims) + dot(al, bh, dims))


def three(a):
    high = a.astype(BF16).astype(F32)
    rest = a - high
    mid = rest.astype(BF16).astype(F32)
    return high, mid, rest - mid


def stacks(x, u):
    def left_of(h, m, l):
        return [h, h, m, h, l, m]

    def right_of(h, m, l):
        return [h, m, h, l, h, m]

    xs, ss, us = three(x), three(x * x), three(u)
    halves = tuple(0.5 * s for s in ss)
    ends = [jnp.ones_like(u), jnp.zeros_like(u)]
    cat = lambda parts: jnp.concatenate(parts, 0).astype(BF16)
    return (
        cat(left_of(*xs)),
        cat(right_of(*xs)),
        cat(left_of(*halves) + left_of(*us) + ends),
        cat(right_of(*ss) + right_of(*us) + ends),
    )


def kernel_block(a, b):
    g = dot(a[0], b[1], TN)
    return g + dot(a[2], b[3], TN) + 0.5 * (g * g)


def add_diagonal(block):
    row = lax.broadcasted_iota(jnp.int32, block.shape, 0)
    col = lax.broadcasted_iota(jnp.int32, block.shape, 1)
    return block + jnp.where(row == col, rho * M, 0.0)


def invert(load, store, n=128, w=8):
    tiles = n // 8
    lane = lax.broadcasted_iota(jnp.int32, (8, n), 1)
    sub = lax.broadcasted_iota(jnp.int32, (8, n), 0)
    a = [load(t) for t in range(tiles)]
    wt = w // 8
    for j in range(n // w):
        k0 = w * j
        mine = range(wt * j, wt * j + wt)
        rest = [t % tiles for t in range(wt * j + wt, wt * j + tiles)]
        inside = (lane >= k0) & (lane < k0 + w)
        cols = {}
        for group in (list(mine), rest[:wt], rest[wt:]):
            for k in range(w):
                for t in group:
                    cols[t, k] = jnp.broadcast_to(a[t][:, k0 + k:k0 + k + 1], (8, n))
        held = {(t, k): cols[t, k] + 0.0 for t in mine for k in range(w)}
        def row_of(x, i):
            return jnp.broadcast_to(x[i:i + 1, :], (8, n))
        e = {(i, k): row_of(held[wt * j + i // 8, k], i % 8) for k in range(w) for i in range(k, w)}
        rows = [row_of(a[wt * j + i // 8], i % 8) for i in range(w)]
        rows = [jnp.where(inside, (lane == k0 + i).astype(F32), rows[i]) for i in range(w)]
        low = {}
        inv = []
        for k in range(w):
            inv.append(1.0 / e[k, k])
            if k + 1 < w:
                e[k + 1, k + 1] = e[k + 1, k + 1] - (e[k + 1, k] * e[k + 1, k]) * inv[k]
            for i in range(k + 1, w):
                low[i, k] = e[i, k] * inv[k]
            for m in range(k + 1, w):
                for i in range(m, w):
                    if i > k + 1:
                        e[i, m] = e[i, m] - low[i, k] * e[m, k]
            for i in range(k + 1, w):
                rows[i] = rows[i] - low[i, k] * rows[k]
        for k in range(w - 1, -1, -1):
            rows[k] = rows[k] * inv[k]
        for i in range(w - 1, 0, -1):
            for k in range(i):
                rows[k] = rows[k] - low[i, k] * rows[i]
        for t in rest:
            new = jnp.where(inside, 0.0, a[t])
            for k in range(w):
                new = new - cols[t, k] * rows[k]
            a[t] = new
        for t in mine:
            new = rows[8 * (t - wt * j)]
            for i in range(1, 8):
                new = jnp.where(sub == i, rows[8 * (t - wt * j) + i], new)
            a[t] = new
    for t in range(tiles):
        store(t, a[t])


def write_features(phi_ref, x_ref, u, at):
    cols = pl.ds(at, MINE)
    phi_ref[0:R, cols] = x_ref[...]
    off = R
    for i in range(R):
        phi_ref[off:off + R - i, cols] = x_ref[i:i + 1, :] * x_ref[i:R, :]
        off += R - i
    phi_ref[off:off + 1, cols] = u
    phi_ref[off + 1:off + 2, cols] = jnp.ones_like(u)
    phi_ref[off + 2:WIDE, cols] = jnp.zeros((WIDE - FEATS, MINE), F32)


def to_chunks(whole, main_ref, ext_ref):
    def piece(r, n, c):
        return whole[r:r + n, 128 * c:128 * c + 128]

    for c in range(7):
        main_ref[2 * c] = piece(0, 8, c)
        main_ref[2 * c + 1] = piece(8, 8, c)
    main_ref[14] = jnp.concatenate([piece(16, 4, 0), piece(16, 4, 1)], 0)
    main_ref[15] = jnp.concatenate([piece(16, 4, 2), piece(16, 4, 3)], 0)
    for i in range(12):
        ext_ref[i] = piece(16 + i % 4, 1, 4 + i // 4)
    for i in range(12, 16):
        ext_ref[i] = jnp.zeros((1, 128), F32)


def from_chunks(main_ref, ext_ref):
    columns = []
    for c in range(7):
        if c < 4:
            last = main_ref[14 + c // 2][4 * (c % 2):4 * (c % 2) + 4, :]
        else:
            last = jnp.concatenate([ext_ref[4 * (c - 4) + i] for i in range(4)], 0)
        columns.append(jnp.concatenate([main_ref[2 * c], main_ref[2 * c + 1], last], 0))
    return jnp.concatenate(columns, 1)


def rows_sum(main, ext):
    return jnp.sum(main, 0, keepdims=True) + ext


def kernel(
    x_ref, u_ref, t_ref, lo_ref, du_ref, co_ref, rh_ref,
    xo, uo, to, phi, phi_h, phi_l, s_ref, d_ref, p_ref, b_h, b_l, l1_ref,
    out_main, out_ext, in_main, in_ext, mid_main, mid_ext, z_main, z_ext, res,
    pair_sems, send1, recv1, send2, recv2, send3, recv3, send_res, recv_res,
):
    slab = lax.axis_index("slab")
    feat = lax.axis_index("feat")
    plane = lax.rem(slab, PLANE)
    depth = lax.div(slab, PLANE)
    other = 1 - feat

    def in_plane(i):
        return depth * PLANE + i

    def in_depth(i):
        return i * PLANE + plane

    barrier = pltpu.get_barrier_semaphore()

    def greet(s, f):
        pl.semaphore_signal(barrier, inc=1, device_id=(s, f), device_id_type=MESH)

    def greet_plane(d, carry):
        peer = in_plane(lax.rem(plane + d, PLANE))
        greet(peer, feat)
        greet(peer, other)
        return carry

    def greet_depth(d, carry):
        greet(in_depth(lax.rem(depth + d, DEPTH)), feat)
        return carry

    greet(slab, other)
    lax.fori_loop(1, PLANE, greet_plane, 0)
    lax.fori_loop(1, DEPTH, greet_depth, 0)

    u_own = u_ref[...]
    own = stacks(x_ref[...], u_own)
    s_ref[0:MINE, 0:MINE] = add_diagonal(kernel_block(own, own))
    write_features(phi, x_ref, u_own, 0)

    pl.semaphore_wait(barrier, 2 * (PLANE - 1) + DEPTH)
    pair = [
        pltpu.make_async_remote_copy(
            src_ref=src, dst_ref=dst, send_sem=pair_sems.at[i], recv_sem=pair_sems.at[3 + i],
            device_id=(slab, other), device_id_type=MESH,
        )
        for i, (src, dst) in enumerate(((x_ref, xo), (u_ref, uo), (t_ref, to)))
    ]
    for copy in pair:
        copy.start()

    def eliminate(kb, carry):
        rows = pl.ds(pl.multiple_of(kb * 128, 128), 128)
        d_ref[...] = s_ref[rows, rows]
        invert(lambda t: d_ref[8 * t:8 * t + 8, :], lambda t, v: d_ref.__setitem__((slice(8 * t, 8 * t + 8), slice(None)), v))

        @pl.when(kb == 0)
        def _():
            for copy in pair:
                copy.wait()
            u_far = uo[...]
            mine = stacks(x_ref[...], u_ref[...])
            far = stacks(xo[...], u_far)
            s_ref[0:MINE, MINE:M] = kernel_block(mine, far)
            s_ref[MINE:M, 0:MINE] = kernel_block(far, mine)
            s_ref[MINE:M, MINE:M] = add_diagonal(kernel_block(far, far))
            write_features(phi, xo, u_far, MINE)

        inverse = d_ref[...]
        p_ref[...] = dot3(two(inverse), two(s_ref[rows, :]), NN)
        p_ref[:, rows] = inverse
        column = two(s_ref[:, rows])
        s_ref[:, rows] = jnp.zeros((M, 128), F32)
        row = two(p_ref[...])
        for rb in range(4):
            part = tuple(c[128 * rb:128 * rb + 128] for c in column)
            s_ref[128 * rb:128 * rb + 128, :] -= dot3(part, row, NN)
        s_ref[rows, :] = p_ref[...]
        return carry

    lax.fori_loop(0, 4, eliminate, 0)

    high, low = two(phi[...])
    phi_h[...] = high
    phi_l[...] = low
    phis = (phi_h, phi_l)

    def with_phi(a, dims):
        return dot3(two(a), (phi_h[...], phi_l[...]), dims)

    first = feat == 0
    targets = jnp.concatenate(
        [jnp.where(first, t[0:HALF, :], t[HALF:R, :]) for t in (t_ref, to)], 1
    )
    inverse = two(s_ref[...])
    w1 = dot3(two(targets), inverse, NN)
    l1 = with_phi(w1, NT)
    l1_ref[...] = l1

    def both(main_src, main_dst, ext_src, ext_dst, send, recv, to_, from_, device):
        return [
            pltpu.make_async_remote_copy(
                src_ref=src, dst_ref=dst, send_sem=send.at[i, to_], recv_sem=recv.at[i, from_],
                device_id=device, device_id_type=MESH,
            )
            for i, (src, dst) in enumerate(((main_src, main_dst), (ext_src, ext_dst)))
        ]

    def scatter(k, peer, at):
        return both(
            out_main.at[k, peer], in_main.at[k, at], out_ext.at[k, peer], in_ext.at[k, at],
            send1.at[k], recv1.at[k], peer, at, (in_plane(peer), feat),
        )

    def across(k, peer, at):
        return both(
            mid_main.at[k, depth], mid_main.at[k, at], mid_ext.at[k, depth], mid_ext.at[k, at],
            send2.at[k], recv2.at[k], peer, at, (in_depth(peer), feat),
        )

    def gather(k, peer, at):
        return both(
            z_main.at[k, plane], z_main.at[k, at], z_ext.at[k, plane], z_ext.at[k, at],
            send3.at[k], recv3.at[k], peer, at, (in_plane(peer), feat),
        )

    def residuals(to_, core, at):
        return pltpu.make_async_remote_copy(
            src_ref=res.at[feat * PLANE + plane], dst_ref=res.at[at],
            send_sem=send_res.at[core * PLANE + to_], recv_sem=recv_res.at[at],
            device_id=(in_plane(to_), core), device_id_type=MESH,
        )

    def start(make, k, me, count):
        def body(d, carry):
            for copy in make(k, lax.rem(me + d, count), me):
                copy.start()
            return carry
        lax.fori_loop(1, count, body, 0)

    def finish(make, k, me, count):
        def body(d, carry):
            peer = lax.rem(me + d, count)
            for copy in make(k, peer, peer):
                copy.wait()
            return carry
        lax.fori_loop(1, count, body, 0)

    def send_chunks(k, whole):
        to_chunks(whole, out_main.at[k], out_ext.at[k])
        start(scatter, k, plane, PLANE)
        in_main[k, plane] = out_main[k, plane]
        in_ext[k, plane] = out_ext[k, plane]

    def squares(pairs, mean):
        total = [jnp.zeros((8, 128), F32), jnp.zeros((1, 128), F32)]
        for piece in pairs:
            for i in range(2):
                gap = piece[i] - mean[i]
                total[i] = total[i] + gap * gap
        return rows_sum(*total)

    def plane_sum(pieces):
        return [functools.reduce(jnp.add, [p[i] for p in pieces]) for i in range(2)]

    def slabs_of(k):
        sent = [(in_main[k, s], in_ext[k, s]) for s in range(PLANE)]
        if k == 0:
            return sent, sent
        before = [(in_main[0, s], in_ext[0, s]) for s in range(PLANE)]
        mean = z_main[0, plane], z_ext[0, plane]
        return sent, [tuple(p - (b - z) for p, b, z in zip(new, old, mean)) for new, old in zip(sent, before)]

    def average(k):
        finish(scatter, k, plane, PLANE)
        sent, operators = slabs_of(k)
        total = plane_sum(sent)
        mean = total if k == 0 else plane_sum(operators)
        mid_main[k, depth] = total[0]
        mid_ext[k, depth] = jnp.concatenate(
            [total[1], squares(operators, [m / PLANE for m in mean])], 0
        )
        start(across, k, depth, DEPTH)

    def conclude(k):
        finish(across, k, depth, DEPTH)
        sums = [(mid_main[k, z], mid_ext[k, z][0:1, :]) for z in range(DEPTH)]
        mean = [m / N_SLAB for m in plane_sum(sums)]
        z_main[k, plane] = mean[0]
        z_ext[k, plane] = mean[1]
        start(gather, k, plane, PLANE)
        if k == 0:
            layers, last = sums, [jnp.zeros((8, 128), F32), jnp.zeros((1, 128), F32)]
        else:
            last = [z_main[0, plane], z_ext[0, plane]]
            old = [(mid_main[0, z], mid_ext[0, z][0:1, :]) for z in range(DEPTH)]
            layers = [tuple(p - (b - PLANE * m) for p, b, m in zip(new, before, last)) for new, before in zip(sums, old)]
        primal = PLANE * squares([tuple(p / PLANE for p in layer) for layer in layers], mean)
        for z in range(DEPTH):
            primal = primal + mid_ext[k, z][1:2, :]
        dual = N_SLAB * rho * rho * squares([mean], last)
        return jnp.sum(primal, 1, keepdims=True), jnp.sum(dual, 1, keepdims=True)

    send_chunks(0, l1)
    rest = two(w1 - rho * M * dot3(two(w1), inverse, NN))
    fixed = dot3(rest, (phi_h[...], phi_l[...]), NT)
    average(0)
    high, low = two(dot3(inverse, (phi_h[...], phi_l[...]), NT))
    b_h[...] = high
    b_l[...] = low
    primal1, dual1 = conclude(0)
    finish(gather, 0, plane, PLANE)
    z1 = from_chunks(z_main.at[0], z_ext.at[0])
    y = two(with_phi(z1, NN))
    l2 = 2.0 * z1 + (fixed - 2.0 * dot3(y, (b_h[...], b_l[...]), NN))
    u1 = l1_ref[...] - z1
    send_chunks(1, l2 + u1)
    lo_ref[0] = l2[:, 0:FEATS]
    u2 = u1 + l2
    average(1)
    primal2, dual2 = conclude(1)
    lane = lax.broadcasted_iota(jnp.int32, (1, 128), 1)
    packed = jnp.zeros((1, 128), F32)
    for i, v in enumerate((primal1, primal2, dual1, dual2)):
        packed = jnp.where(lane == i, v, packed)
    spot = feat * PLANE + plane
    res[spot] = packed
    residuals(plane, other, spot).start()

    def send_residuals(d, carry):
        peer = lax.rem(plane + d, PLANE)
        residuals(peer, feat, spot).start()
        residuals(peer, other, spot).start()
        return carry

    lax.fori_loop(1, PLANE, send_residuals, 0)
    finish(gather, 1, plane, PLANE)
    z2 = from_chunks(z_main.at[1], z_ext.at[1])
    du_ref[0] = (u2 - z2)[:, 0:FEATS]
    co_ref[...] = z2[:, 0:FEATS]
    residuals(plane, other, other * PLANE + plane).wait()

    def wait_residuals(d, carry):
        peer = lax.rem(plane + d, PLANE)
        residuals(peer, feat, feat * PLANE + peer).wait()
        residuals(peer, other, other * PLANE + peer).wait()
        return carry

    lax.fori_loop(1, PLANE, wait_residuals, 0)
    total = functools.reduce(jnp.add, [res[i] for i in range(2 * PLANE)])
    total = jnp.sqrt(total / (N_SLAB * R * FEATS))
    rh_ref[...] = jnp.concatenate([total[:, 0:2], total[:, 2:4]], 0)


def shards(states, inputs, targets):
    vmem = pl.BlockSpec(memory_space=pltpu.VMEM)
    dma = pltpu.SemaphoreType.DMA
    f32 = lambda *shape: pltpu.VMEM(shape, F32)
    half = lambda *shape: pltpu.VMEM(shape, BF16)
    return pl.pallas_call(
        kernel,
        out_shape=(
            jax.ShapeDtypeStruct((1, HALF, FEATS), F32),
            jax.ShapeDtypeStruct((1, HALF, FEATS), F32),
            jax.ShapeDtypeStruct((HALF, FEATS), F32),
            jax.ShapeDtypeStruct((2, 2), F32),
        ),
        in_specs=[vmem] * 3,
        out_specs=(vmem,) * 4,
        scratch_shapes=[
            f32(R, MINE), f32(1, MINE), f32(R, MINE),
            f32(WIDE, M), half(WIDE, M), half(WIDE, M), f32(M, M), f32(128, 128), f32(128, M),
            half(M, WIDE), half(M, WIDE), f32(HALF, WIDE),
            f32(2, PLANE, 8, 128), f32(2, PLANE, 1, 128), f32(2, PLANE, 8, 128), f32(2, PLANE, 1, 128),
            f32(2, DEPTH, 8, 128), f32(2, DEPTH, 2, 128),
            f32(2, PLANE, 8, 128), f32(2, PLANE, 1, 128), f32(2 * PLANE, 1, 128),
            dma((6,)), dma((2, 2, PLANE)), dma((2, 2, PLANE)), dma((2, 2, DEPTH)), dma((2, 2, DEPTH)),
            dma((2, 2, PLANE)), dma((2, 2, PLANE)), dma((2 * PLANE,)), dma((2 * PLANE,)),
        ],
        compiler_params=pltpu.CompilerParams(
            collective_id=0, has_side_effects=True, vmem_limit_bytes=48 * 1024 * 1024
        ),
        name="consensus",
    )(states, inputs.reshape(1, MINE), targets)


def solution(mesh):
    return jax.shard_map(
        shards,
        mesh=mesh,
        in_specs=(P(None, ("slab", "feat")), P(("slab", "feat")), P(None, ("slab", "feat"))),
        out_specs=(P("slab", "feat", None), P("slab", "feat", None), P("feat", None), P()),
        check_vma=False,
    )
```

time: 667 us -> 69.9 us (0.10)
  waiting for transfers between devices: 259 us -> 0 us
  other arithmetic: 252 us -> 0 us
  Pallas kernels: 0 us -> 64.2 us
  blocking collectives: 45.4 us -> 0 us
  local copies, waits for them, and re-layouts: 46.1 us -> 4.84 us
  matrix products: 37.7 us -> 0 us
  between operations: 20 us -> 0.65 us
    all_gather x2 -> x0, waiting for transfers between devices: 259 us -> none  [total_of_pieces(): tiles = lax.all_gather(array, axis)]
    another operation x36 -> x0, other arithmetic: 224 us -> none  [the longest x26 149 us: shards(): jnp.linalg.cholesky(gram_matrix + penalty * jnp.eye(width, dtype=jnp.floa...]
    pallas_call x0 -> x1, Pallas kernels: none -> 64.2 us  [shards(): pl.pallas_call(kernel, out_shape=(jax.ShapeDtypeStruct((1, HALF, FEATS),...]
    psum x4 -> x0, blocking collectives: 40.7 us -> none  [by_axis(): array = lax.psum(array, axis)]
    another operation x64 -> x0, matrix products: 26.8 us -> none  [the longest x12 13.7 us: shards(): jnp.linalg.cholesky(gram_matrix + penalty * jnp.eye(width, dtype=jnp.floa...]
    another operation x35 -> x0, local copies, waits for them, and re-layouts: 21.2 us -> none  [the longest x26 19.2 us: solve_rows(): return jax.scipy.linalg.cho_solve((factor, True), right_side.T).T]
    concatenate x1 -> x0, local copies, waits for them, and re-layouts: 13.3 us -> none  [features(): return jnp.concatenate(blocks, 0)]
    reduce_sum x3 -> x0, other arithmetic: 11.7 us -> none  [the longest x2 10.1 us: total_of_pieces(): return tiles.sum(axis=0)]
  transfers between devices with their start and end apart: 2 -> 0, of which waited for: 2 -> 0; matrix products, arithmetic and copies ran while one was open for 0% -> 0% of each run, Pallas kernels for 0% -> 0%
where the time goes in v1:
time: 69.9 us; the launch traced here: 69.6 us
  Pallas kernels  64.2 us (92%)
  local copies, waits for them, and re-layouts  4.84 us (7%)
    pallas_call x1, Pallas kernels, shards(): pl.pallas_call(kernel, out_shape=(jax.ShapeDtypeStruct((1, HALF, FEATS),...  64.2 us
    unnamed x8, local copies, waits for them, and re-layouts  3.43 us
    pallas_call x2, local copies, waits for them, and re-layouts, shards(): pl.pallas_call(kernel, out_shape=(jax.ShapeDtypeStruct((1, HALF, FEATS),...  1.41 us

profile of v1, /device:TPU:1, one launch (start us, length us, event | category | flops | bytes accessed | tf_op | source)
XLA Modules:
  0.0 69.6 jit_solution(17705761498898392993)
XLA Ops:
  0.6 0.0 copy-start.2
  0.6 0.7 copy-done.2
  1.3 0.0 copy-start
  1.3 0.8 %copy-done = f32[40,256]{1,0:T(8,128)S(1)} copy-done((f32[40,256]{1,0:T(8,128)S(1)}, f32[40,256]{1,0:T(8,128)}, u32[]{:S(2)}) %copy-start) | copy-done | bytes 40984
  2.1 0.0 copy-start.1
  2.1 0.8 %copy-done.1 = f32[40,256]{1,0:T(8,128)S(1)} copy-done((f32[40,256]{1,0:T(8,128)S(1)}, f32[40,256]{1,0:T(8,128)}, u32[]{:S(2)}) %copy-start.1) | copy-done | bytes 40984
  2.9 64.2 %consensus.1 = (f32[1,20,862]{2,1,0:T(8,128)S(1)}, f32[1,20,862]{2,1,0:T(8,128)S(1)}, f32[20,862]{1,0:T(8,128)S(1)}, f32[2,2]{1,0:T(2,128)S(1)}) custom-call(f32[40,256]{1,0:T(8,128)S(1)} %copy-done, f32[1,256]{1,0:T(1,128)S(1)} %bitcast.1, f32[40,256]{1,0:T(8,128)S(1)} %copy-done.1), custom_call_target="tpu_custom_call" | custom-call | tf_op jit(solution)/shard_map/consensus/pallas_call | solution.py:437
  67.0 0.7 %copy.7 = f32[1,20,862]{2,0,1:T(1,128)} copy(f32[1,20,862]{2,1,0:T(8,128)S(1)} %get-tuple-element.4) | data formatting | bytes 137920 | tf_op jit(solution)/shard_map/consensus/pallas_call | solution.py:437
  67.7 0.7 %copy.8 = f32[1,20,862]{2,0,1:T(1,128)} copy(f32[1,20,862]{2,1,0:T(8,128)S(1)} %get-tuple-element.5) | data formatting | bytes 137920 | tf_op jit(solution)/shard_map/consensus/pallas_call | solution.py:437
  68.5 0.6 copy.11
  69.1 0.6 copy.12
Async XLA Ops:
  0.6 0.7 copy-start.2
  1.3 0.8 %copy-start = (f32[40,256]{1,0:T(8,128)S(1)}, f32[40,256]{1,0:T(8,128)}, u32[]{:S(2)}) copy-start(f32[40,256]{1,0:T(8,128)} %x_ref.1) | copy-start | bytes 122884
  2.1 0.8 %copy-start.1 = (f32[40,256]{1,0:T(8,128)S(1)}, f32[40,256]{1,0:T(8,128)}, u32[]{:S(2)}) copy-start(f32[40,256]{1,0:T(8,128)} %t_ref.1) | copy-start | bytes 122884

commit v2 on v1

v2 whole, which is shorter than its diff:
```python
import functools

import jax
import jax.numpy as jnp
from jax import lax
from jax.experimental import pallas as pl
from jax.experimental.pallas import tpu as pltpu
from jax.sharding import PartitionSpec as P

F32, BF16 = jnp.float32, jnp.bfloat16
NN = (((1,), (0,)), ((), ()))
NT = (((1,), (1,)), ((), ()))
TN = (((0,), (0,)), ((), ()))
MESH = pl.DeviceIdType.MESH

R = 40
HALF = 20
FEATS = 862
WIDE = 896
PLANE = 16
DEPTH = 8
N_SLAB = 128
M = 512
MINE = 256
rho = 1.0


def dot(a, b, dims):
    return lax.dot_general(a, b, dims, preferred_element_type=F32)


def two(a):
    high = a.astype(BF16)
    return high, (a - high.astype(F32)).astype(BF16)


def dot3(a, b, dims):
    (ah, al), (bh, bl) = a, b
    return dot(ah, bh, dims) + (dot(ah, bl, dims) + dot(al, bh, dims))


def three(a):
    high = a.astype(BF16).astype(F32)
    rest = a - high
    mid = rest.astype(BF16).astype(F32)
    return high, mid, rest - mid


def stacks(x, u):
    def left_of(h, m, l):
        return [h, h, m, h, l, m]

    def right_of(h, m, l):
        return [h, m, h, l, h, m]

    xs, ss, us = three(x), three(x * x), three(u)
    halves = tuple(0.5 * s for s in ss)
    ends = [jnp.ones_like(u), jnp.zeros_like(u)]
    cat = lambda parts: jnp.concatenate(parts, 0).astype(BF16)
    return (
        cat(left_of(*xs)),
        cat(right_of(*xs)),
        cat(left_of(*halves) + left_of(*us) + ends),
        cat(right_of(*ss) + right_of(*us) + ends),
    )


def kernel_block(a, b):
    g = dot(a[0], b[1], TN)
    return g + dot(a[2], b[3], TN) + 0.5 * (g * g)


def add_diagonal(block):
    row = lax.broadcasted_iota(jnp.int32, block.shape, 0)
    col = lax.broadcasted_iota(jnp.int32, block.shape, 1)
    return block + jnp.where(row == col, rho * M, 0.0)


def invert(load, store, n=128, w=8):
    tiles, wt = n // 8, w // 8
    lane = lax.broadcasted_iota(jnp.int32, (8, n), 1)
    sub = lax.broadcasted_iota(jnp.int32, (8, n), 0)

    def row_of(x, i):
        return jnp.broadcast_to(x[i:i + 1, :], (8, n))

    a = [load(t) for t in range(tiles)]
    for j in range(n // w):
        k0, t0 = w * j, wt * j
        rest = [t % tiles for t in range(t0 + wt, t0 + tiles)]
        inside = (lane >= k0) & (lane < k0 + w)

        def spread(t, k):
            return jnp.broadcast_to(a[t][:, k0 + k:k0 + k + 1], (8, n))

        spreads = {}
        for group in (range(t0, t0 + wt), rest):
            for k in range(w):
                for t in group:
                    spreads[t, k] = spread(t, k)
        col = [[spreads[t0 + s, k] + 0.0 for s in range(wt)] for k in range(w)]
        row = [jnp.where(inside, (lane == k0 + 8 * s + sub).astype(F32), a[t0 + s]) for s in range(wt)]
        scale = [None] * wt
        for k in range(w):
            s0, i = divmod(k, 8)
            inv = 1.0 / row_of(col[k][s0], i)
            scale[s0] = inv if i == 0 else jnp.where(sub == i, inv, scale[s0])
            off = list(col[k])
            off[s0] = jnp.where(sub == i, 0.0, off[s0])
            for m in range(k + 1, w):
                factor = row_of(col[m][s0], i) * inv
                col[m] = [c - o * factor for c, o in zip(col[m], off)]
            factor = row_of(row[s0], i) * inv
            row = [r - o * factor for r, o in zip(row, off)]
        row = [r * s for r, s in zip(row, scale)]
        pivots = [row_of(row[k // 8], k % 8) for k in range(w)]
        for t in rest:
            new = jnp.where(inside, 0.0, a[t])
            for k in range(w):
                new = new - spreads[t, k] * pivots[k]
            a[t] = new
        for s in range(wt):
            a[t0 + s] = row[s]
    for t in range(tiles):
        store(t, a[t])


def write_features(phi_ref, x_ref, u, at):
    cols = pl.ds(at, MINE)
    phi_ref[0:R, cols] = x_ref[...]
    off = R
    for i in range(R):
        phi_ref[off:off + R - i, cols] = x_ref[i:i + 1, :] * x_ref[i:R, :]
        off += R - i
    phi_ref[off:off + 1, cols] = u
    phi_ref[off + 1:off + 2, cols] = jnp.ones_like(u)
    phi_ref[off + 2:WIDE, cols] = jnp.zeros((WIDE - FEATS, MINE), F32)


def to_chunks(whole, out_ref):
    def piece(r, n, c):
        return whole[r:r + n, 128 * c:128 * c + 128]

    for c in range(7):
        out_ref[2 * c, 0:8, :] = piece(0, 8, c)
        out_ref[2 * c + 1, 0:8, :] = piece(8, 8, c)
    out_ref[14, 0:8, :] = jnp.concatenate([piece(16, 4, 0), piece(16, 4, 1)], 0)
    out_ref[15, 0:8, :] = jnp.concatenate([piece(16, 4, 2), piece(16, 4, 3)], 0)
    for i in range(12):
        out_ref[i, 8:9, :] = piece(16 + i % 4, 1, 4 + i // 4)
    for i in range(12, 16):
        out_ref[i, 8:9, :] = jnp.zeros((1, 128), F32)


def from_chunks(ref):
    columns = []
    for c in range(7):
        if c < 4:
            last = ref[14 + c // 2, 4 * (c % 2):4 * (c % 2) + 4, :]
        else:
            last = jnp.concatenate([ref[4 * (c - 4) + i, 8:9, :] for i in range(4)], 0)
        columns.append(jnp.concatenate([ref[2 * c, 0:8, :], ref[2 * c + 1, 0:8, :], last], 0))
    return jnp.concatenate(columns, 1)


def rows_sum(main, ext):
    return jnp.sum(main, 0, keepdims=True) + ext


def kernel(
    x_ref, u_ref, t_ref, lo_ref, du_ref, co_ref, rh_ref,
    xo, uo, to, phi, phi_h, phi_l, s_ref, d_ref, p_ref, b_h, b_l, l1_ref,
    outs, ins, mids, zs, zs_far, res, sent, stats,
    pair_sems, send1, recv1, send2, recv2, send3, recv3, send_res, recv_res,
):
    slab = lax.axis_index("slab")
    feat = lax.axis_index("feat")
    plane = lax.rem(slab, PLANE)
    depth = lax.div(slab, PLANE)
    line, spot = lax.div(plane, 4), lax.rem(plane, 4)
    other = 1 - feat
    owner = feat == 1
    steps = sorted(((dy, dx) for dy in range(4) for dx in range(4) if dy or dx), key=lambda d: -sum(min(v, 4 - v) for v in d))
    far_planes = [4 * lax.rem(line + dy, 4) + lax.rem(spot + dx, 4) for dy, dx in steps]
    far_depths = [lax.rem(depth + d, DEPTH) for d in (4, 3, 5, 2, 6, 1, 7)]

    def in_plane(i):
        return depth * PLANE + i

    def in_depth(i):
        return i * PLANE + plane

    barrier = pltpu.get_barrier_semaphore()

    def greet(s, f):
        pl.semaphore_signal(barrier, inc=1, device_id=(s, f), device_id_type=MESH)

    greet(slab, other)
    for peer in far_planes:
        greet(in_plane(peer), 1)

    @pl.when(owner)
    def _():
        for peer in far_planes:
            greet(in_plane(peer), 0)
        for peer in far_depths:
            greet(in_depth(peer), 1)

    u_own = u_ref[...]
    own = stacks(x_ref[...], u_own)
    s_ref[0:MINE, 0:MINE] = add_diagonal(kernel_block(own, own))
    write_features(phi, x_ref, u_own, 0)

    pl.semaphore_wait(barrier, PLANE + feat * (PLANE + DEPTH - 2))
    pair = [
        pltpu.make_async_remote_copy(
            src_ref=src, dst_ref=dst, send_sem=pair_sems.at[i], recv_sem=pair_sems.at[3 + i],
            device_id=(slab, other), device_id_type=MESH,
        )
        for i, (src, dst) in enumerate(((x_ref, xo), (u_ref, uo), (t_ref, to)))
    ]
    for copy in pair:
        copy.start()

    def eliminate(kb, carry):
        rows = pl.ds(pl.multiple_of(kb * 128, 128), 128)
        d_ref[...] = s_ref[rows, rows]
        invert(lambda t: d_ref[8 * t:8 * t + 8, :], lambda t, v: d_ref.__setitem__((slice(8 * t, 8 * t + 8), slice(None)), v))

        @pl.when(kb == 0)
        def _():
            for copy in pair:
                copy.wait()
            u_far = uo[...]
            mine = stacks(x_ref[...], u_ref[...])
            far = stacks(xo[...], u_far)
            s_ref[0:MINE, MINE:M] = kernel_block(mine, far)
            s_ref[MINE:M, 0:MINE] = kernel_block(far, mine)
            s_ref[MINE:M, MINE:M] = add_diagonal(kernel_block(far, far))
            write_features(phi, xo, u_far, MINE)

        inverse = d_ref[...]
        p_ref[...] = dot3(two(inverse), two(s_ref[rows, :]), NN)
        p_ref[:, rows] = inverse
        column = two(s_ref[:, rows])
        s_ref[:, rows] = jnp.zeros((M, 128), F32)
        row = two(p_ref[...])
        for rb in range(4):
            part = tuple(c[128 * rb:128 * rb + 128] for c in column)
            s_ref[128 * rb:128 * rb + 128, :] -= dot3(part, row, NN)
        s_ref[rows, :] = p_ref[...]
        return carry

    lax.fori_loop(0, 4, eliminate, 0)

    high, low = two(phi[...])
    phi_h[...] = high
    phi_l[...] = low
    phis = (phi_h, phi_l)

    def with_phi(a, dims):
        return dot3(two(a), (phi_h[...], phi_l[...]), dims)

    first = feat == 0
    targets = jnp.concatenate(
        [jnp.where(first, t[0:HALF, :], t[HALF:R, :]) for t in (t_ref, to)], 1
    )
    inverse = two(s_ref[...])
    w1 = dot3(two(targets), inverse, NN)
    l1 = with_phi(w1, NT)
    l1_ref[...] = l1

    def remote(src, dst, send, recv, device):
        return pltpu.make_async_remote_copy(
            src_ref=src, dst_ref=dst, send_sem=send, recv_sem=recv, device_id=device, device_id_type=MESH
        )

    def take(ref, sem):
        pltpu.make_async_copy(ref, ref, sem).wait()

    def send_chunks(k, whole):
        to_chunks(whole, outs.at[k])

        def scatter(peer):
            remote(
                outs.at[k, peer], ins.at[k, feat * PLANE + plane], send1.at[k], recv1.at[k], (in_plane(peer), 1)
            ).start()

        for peer in far_planes:
            scatter(peer)

        @pl.when(owner)
        def _():
            ins[k, PLANE + plane] = outs[k, plane]

        @pl.when(jnp.logical_not(owner))
        def _():
            scatter(plane)

    def parts(ref, *at):
        return [ref[(*at, slice(0, 8))], ref[(*at, slice(8, 9))]]

    def add_up(pieces):
        return [functools.reduce(jnp.add, [p[i] for p in pieces]) for i in range(2)]

    def squares(pieces, mean):
        total = [jnp.zeros((8, 128), F32), jnp.zeros((1, 128), F32)]
        for piece in pieces:
            for i in range(2):
                gap = piece[i] - mean[i]
                total[i] = total[i] + gap * gap
        return jnp.sum(total[0], 0, keepdims=True) + total[1]

    def consensus_of(k, half):
        return parts(zs, k, plane) if half else parts(zs_far, k)

    def layer(k, z, half):
        return [mids[k, z, 8 * half:8 * half + 8, :], mids[k, z, 16 + half:17 + half, :]]

    def average(k):
        take(ins.at[k, 0:2 * PLANE - 1], recv1.at[k])
        spread = jnp.zeros((1, 128), F32)
        for half in range(2):
            sent = [parts(ins, k, PLANE * half + s) for s in range(PLANE)]
            total = mean = add_up(sent)
            operators = sent
            if k == 1:
                last = consensus_of(0, half)
                before = [parts(ins, 0, PLANE * half + s) for s in range(PLANE)]
                operators = [[p - (b - z) for p, b, z in zip(new, old, last)] for new, old in zip(sent, before)]
                mean = add_up(operators)
            mids[k, depth, 8 * half:8 * half + 8, :] = total[0]
            mids[k, depth, 16 + half:17 + half, :] = total[1]
            spread = spread + squares(operators, [m / PLANE for m in mean])
        mids[k, depth, 18:19, :] = spread
        for peer in far_depths:
            remote(
                mids.at[k, depth], mids.at[k, depth], send2.at[k], recv2.at[k], (in_depth(peer), 1)
            ).start()

    def conclude(k):
        take(mids.at[k, 0:DEPTH - 1], recv2.at[k])
        means = []
        for half in range(2):
            means.append([m / N_SLAB for m in add_up([layer(k, z, half) for z in range(DEPTH)])])
        zs_far[k, 0:8, :] = means[0][0]
        zs_far[k, 8:9, :] = means[0][1]
        zs[k, plane, 0:8, :] = means[1][0]
        zs[k, plane, 8:9, :] = means[1][1]

        def gather(src, peer, core):
            remote(src, zs.at[k, plane], send3.at[k], recv3.at[k], (in_plane(peer), core)).start()

        for peer in far_planes:
            gather(zs_far.at[k], peer, 0)
            gather(zs.at[k, plane], peer, 1)
        gather(zs_far.at[k], plane, 0)

    def statistics(k):
        primal = jnp.zeros((1, 128), F32)
        dual = jnp.zeros((1, 128), F32)
        for half in range(2):
            mean = consensus_of(k, half)
            layers = [layer(k, z, half) for z in range(DEPTH)]
            if k == 0:
                last = [jnp.zeros((8, 128), F32), jnp.zeros((1, 128), F32)]
            else:
                last = consensus_of(0, half)
                before = [layer(0, z, half) for z in range(DEPTH)]
                layers = [[p - (b - PLANE * z) for p, b, z in zip(new, old, last)] for new, old in zip(layers, before)]
            primal = primal + PLANE * squares([[p / PLANE for p in each] for each in layers], mean)
            dual = dual + squares([mean], last)
        for z in range(DEPTH):
            primal = primal + mids[k, z, 18:19, :]
        return jnp.sum(primal, 1, keepdims=True), N_SLAB * rho * rho * jnp.sum(dual, 1, keepdims=True)

    def gathered(k):
        @pl.when(owner)
        def _():
            take(zs.at[k, 0:PLANE - 1], recv3.at[k])

        @pl.when(jnp.logical_not(owner))
        def _():
            take(zs.at[k], recv3.at[k])

        return from_chunks(zs.at[k])

    lane = lax.broadcasted_iota(jnp.int32, (1, 128), 1)

    send_chunks(0, l1)
    rest = two(w1 - rho * M * dot3(two(w1), inverse, NN))
    fixed = dot3(rest, (phi_h[...], phi_l[...]), NT)

    @pl.when(owner)
    def _():
        average(0)

    high, low = two(dot3(inverse, (phi_h[...], phi_l[...]), NT))
    b_h[...] = high
    b_l[...] = low

    @pl.when(owner)
    def _():
        conclude(0)
        primal, dual = statistics(0)
        stats[...] = jnp.where(lane == 0, primal, jnp.where(lane == 2, dual, 0.0))

    z1 = gathered(0)
    y = two(with_phi(z1, NN))
    l2 = 2.0 * z1 + (fixed - 2.0 * dot3(y, (b_h[...], b_l[...]), NN))
    u1 = l1_ref[...] - z1
    send_chunks(1, l2 + u1)
    lo_ref[0] = l2[:, 0:FEATS]
    l1_ref[...] = u1 + l2

    @pl.when(owner)
    def _():
        average(1)
        conclude(1)
        primal, dual = statistics(1)
        res[plane] = jnp.where(lane == 1, primal, jnp.where(lane == 3, dual, stats[...]))
        for peer in far_planes:
            for core in range(2):
                remote(res.at[plane], res.at[plane], send_res.at[0], recv_res.at[0], (in_plane(peer), core)).start()
        remote(res.at[plane], res.at[plane], send_res.at[0], recv_res.at[0], (slab, 0)).start()

    z2 = gathered(1)
    du_ref[0] = (l1_ref[...] - z2)[:, 0:FEATS]
    co_ref[...] = z2[:, 0:FEATS]

    @pl.when(owner)
    def _():
        take(res.at[0:PLANE - 1], recv_res.at[0])

    @pl.when(jnp.logical_not(owner))
    def _():
        take(res, recv_res.at[0])

    total = functools.reduce(jnp.add, [res[i] for i in range(PLANE)])
    total = jnp.sqrt(total / (N_SLAB * R * FEATS))
    rh_ref[...] = jnp.concatenate([total[:, 0:2], total[:, 2:4]], 0)

    @pl.when(owner)
    def _():
        for k in range(2):
            take(outs.at[k, 0:PLANE - 1], send1.at[k])
            take(mids.at[k, 0:DEPTH - 1], send2.at[k])
            take(ins.at[k, 0:2 * PLANE - 1], send3.at[k])
        take(sent.at[0:2 * PLANE - 1], send_res.at[0])

    @pl.when(jnp.logical_not(owner))
    def _():
        for k in range(2):
            take(outs.at[k], send1.at[k])


def shards(states, inputs, targets):
    vmem = pl.BlockSpec(memory_space=pltpu.VMEM)
    dma = pltpu.SemaphoreType.DMA
    f32 = lambda *shape: pltpu.VMEM(shape, F32)
    half = lambda *shape: pltpu.VMEM(shape, BF16)
    return pl.pallas_call(
        kernel,
        out_shape=(
            jax.ShapeDtypeStruct((1, HALF, FEATS), F32),
            jax.ShapeDtypeStruct((1, HALF, FEATS), F32),
            jax.ShapeDtypeStruct((HALF, FEATS), F32),
            jax.ShapeDtypeStruct((2, 2), F32),
        ),
        in_specs=[vmem] * 3,
        out_specs=(vmem,) * 4,
        scratch_shapes=[
            f32(R, MINE), f32(1, MINE), f32(R, MINE),
            f32(WIDE, M), half(WIDE, M), half(WIDE, M), f32(M, M), f32(128, 128), f32(128, M),
            half(M, WIDE), half(M, WIDE), f32(HALF, WIDE),
            f32(2, PLANE, 9, 128), f32(2, 2 * PLANE, 9, 128), f32(2, DEPTH, 19, 128),
            f32(2, PLANE, 9, 128), f32(2, 9, 128), f32(PLANE, 1, 128), f32(2 * PLANE, 1, 128), f32(1, 128),
            dma((6,)), dma((2,)), dma((2,)), dma((2,)), dma((2,)), dma((2,)), dma((2,)), dma((1,)), dma((1,)),
        ],
        compiler_params=pltpu.CompilerParams(
            collective_id=0, has_side_effects=True, vmem_limit_bytes=48 * 1024 * 1024
        ),
        name="consensus",
    )(states, inputs.reshape(1, MINE), targets)


def solution(mesh):
    return jax.shard_map(
        shards,
        mesh=mesh,
        in_specs=(P(None, ("slab", "feat")), P(("slab", "feat")), P(None, ("slab", "feat"))),
        out_specs=(P("slab", "feat", None), P("slab", "feat", None), P("feat", None), P()),
        check_vma=False,
    )
```

time: 69.9 us -> 61.2 us (0.88)
  Pallas kernels: 64.2 us -> 55.5 us
    pallas_call x1, Pallas kernels: 64.2 us -> 55.5 us  [shards(): pl.pallas_call(kernel, out_shape=(jax.ShapeDtypeStruct((1, HALF, FEATS),...]
where the time goes in v2:
time: 61.2 us; the launch traced here: 61 us
  Pallas kernels  55.5 us (91%)
  local copies, waits for them, and re-layouts  4.84 us (8%)
  between operations  0.65 us (1%)
    pallas_call x1, Pallas kernels, shards(): pl.pallas_call(kernel, out_shape=(jax.ShapeDtypeStruct((1, HALF, FEATS),...  55.5 us
    unnamed x8, local copies, waits for them, and re-layouts  3.43 us
    pallas_call x2, local copies, waits for them, and re-layouts, shards(): pl.pallas_call(kernel, out_shape=(jax.ShapeDtypeStruct((1, HALF, FEATS),...  1.41 us

profile of v2, /device:TPU:1, one launch (start us, length us, event | category | flops | bytes accessed | tf_op | source)
XLA Modules:
  0.0 61.0 jit_solution(16237256568520326337)
XLA Ops:
  0.6 0.0 copy-start.2
  0.6 0.7 %copy-done.2 = f32[256]{0:T(256)S(1)} copy-done((f32[256]{0:T(256)S(1)}, f32[256]{0:T(256)}, u32[]{:S(2)}) %copy-start.2) | copy-done | bytes 1048
  1.3 0.0 copy-start
  1.3 0.8 %copy-done = f32[40,256]{1,0:T(8,128)S(1)} copy-done((f32[40,256]{1,0:T(8,128)S(1)}, f32[40,256]{1,0:T(8,128)}, u32[]{:S(2)}) %copy-start) | copy-done | bytes 40984
  2.1 0.0 copy-start.1
  2.1 0.8 %copy-done.1 = f32[40,256]{1,0:T(8,128)S(1)} copy-done((f32[40,256]{1,0:T(8,128)S(1)}, f32[40,256]{1,0:T(8,128)}, u32[]{:S(2)}) %copy-start.1) | copy-done | bytes 40984
  2.9 55.5 %consensus.1 = (f32[1,20,862]{2,1,0:T(8,128)S(1)}, f32[1,20,862]{2,1,0:T(8,128)S(1)}, f32[20,862]{1,0:T(8,128)S(1)}, f32[2,2]{1,0:T(2,128)S(1)}) custom-call(f32[40,256]{1,0:T(8,128)S(1)} %copy-done, f32[1,256]{1,0:T(1,128)S(1)} %bitcast.1, f32[40,256]{1,0:T(8,128)S(1)} %copy-done.1), custom_call_target="tpu_custom_call" | custom-call | tf_op jit(solution)/shard_map/consensus/pallas_call | solution.py:462
  58.4 0.7 %copy.7 = f32[1,20,862]{2,0,1:T(1,128)} copy(f32[1,20,862]{2,1,0:T(8,128)S(1)} %get-tuple-element.4) | data formatting | bytes 137920 | tf_op jit(solution)/shard_map/consensus/pallas_call | solution.py:462
  59.1 0.7 %copy.8 = f32[1,20,862]{2,0,1:T(1,128)} copy(f32[1,20,862]{2,1,0:T(8,128)S(1)} %get-tuple-element.5) | data formatting | bytes 137920 | tf_op jit(solution)/shard_map/consensus/pallas_call | solution.py:462
  59.8 0.6 %copy.11 = f32[20,862]{1,0:T(8,128)} copy(f32[20,862]{1,0:T(8,128)S(1)} %get-tuple-element.14) | data formatting | bytes 137920
  60.5 0.6 copy.12
Async XLA Ops:
  0.6 0.7 %copy-start.2 = (f32[256]{0:T(256)S(1)}, f32[256]{0:T(256)}, u32[]{:S(2)}) copy-start(f32[256]{0:T(256)} %param.4) | copy-start | bytes 3076
  1.3 0.8 %copy-start = (f32[40,256]{1,0:T(8,128)S(1)}, f32[40,256]{1,0:T(8,128)}, u32[]{:S(2)}) copy-start(f32[40,256]{1,0:T(8,128)} %x_ref.1) | copy-start | bytes 122884
  2.1 0.8 %copy-start.1 = (f32[40,256]{1,0:T(8,128)S(1)}, f32[40,256]{1,0:T(8,128)}, u32[]{:S(2)}) copy-start(f32[40,256]{1,0:T(8,128)} %t_ref.1) | copy-start | bytes 122884

commit v3 on v2

--- a/solution.py
+++ b/solution.py
@@ -39,6 +39,17 @@
     return dot(ah, bh, dims) + (dot(ah, bl, dims) + dot(al, bh, dims))
 
 
+def rows3(a, b, dims):
+    rows, pad = a.shape[0], -a.shape[0] % 8
+    if pad:
+        a = jnp.concatenate([a, jnp.zeros((pad, a.shape[1]), F32)], 0)
+    tall = rows + pad
+    high = a.astype(BF16).astype(F32)
+    both = jnp.concatenate([high, a - high], 0).astype(BF16)
+    first = dot(both, b[0], dims)
+    return (first[0:tall] + (first[tall:] + dot(high.astype(BF16), b[1], dims)))[0:rows]
+
+
 def three(a):
     high = a.astype(BF16).astype(F32)
     rest = a - high
@@ -76,7 +87,7 @@
     return block + jnp.where(row == col, rho * M, 0.0)
 
 
-def invert(load, store, n=128, w=8):
+def invert(a, n=128, w=16):
     tiles, wt = n // 8, w // 8
     lane = lax.broadcasted_iota(jnp.int32, (8, n), 1)
     sub = lax.broadcasted_iota(jnp.int32, (8, n), 0)
@@ -84,21 +95,18 @@
     def row_of(x, i):
         return jnp.broadcast_to(x[i:i + 1, :], (8, n))
 
-    a = [load(t) for t in range(tiles)]
+    a = [a[8 * t:8 * t + 8] for t in range(tiles)]
     for j in range(n // w):
         k0, t0 = w * j, wt * j
-        rest = [t % tiles for t in range(t0 + wt, t0 + tiles)]
+        near = [t % tiles for t in range(t0 + wt, t0 + 2 * wt)] if j + 1 < n // w else []
+        rest = [t for t in range(tiles) if t not in near and not t0 <= t < t0 + wt]
         inside = (lane >= k0) & (lane < k0 + w)
 
         def spread(t, k):
             return jnp.broadcast_to(a[t][:, k0 + k:k0 + k + 1], (8, n))
 
-        spreads = {}
-        for group in (range(t0, t0 + wt), rest):
-            for k in range(w):
-                for t in group:
-                    spreads[t, k] = spread(t, k)
-        col = [[spreads[t0 + s, k] + 0.0 for s in range(wt)] for k in range(w)]
+        col = [[spread(t0 + s, k) + 0.0 for s in range(wt)] for k in range(w)]
+        ahead = {(t, k): spread(t, k) for k in range(w) for t in near}
         row = [jnp.where(inside, (lane == k0 + 8 * s + sub).astype(F32), a[t0 + s]) for s in range(wt)]
         scale = [None] * wt
         for k in range(w):
@@ -108,21 +116,36 @@
             off = list(col[k])
             off[s0] = jnp.where(sub == i, 0.0, off[s0])
             for m in range(k + 1, w):
-                factor = row_of(col[m][s0], i) * inv
-                col[m] = [c - o * factor for c, o in zip(col[m], off)]
+                factor = row_of(col[m][s0], i)
+                if m == k + 1:
+                    col[m] = [c - (o * factor) * inv for c, o in zip(col[m], off)]
+                else:
+                    factor = factor * inv
+                    col[m] = [c - o * factor for c, o in zip(col[m], off)]
             factor = row_of(row[s0], i) * inv
             row = [r - o * factor for r, o in zip(row, off)]
         row = [r * s for r, s in zip(row, scale)]
-        pivots = [row_of(row[k // 8], k % 8) for k in range(w)]
-        for t in rest:
-            new = jnp.where(inside, 0.0, a[t])
-            for k in range(w):
-                new = new - spreads[t, k] * pivots[k]
-            a[t] = new
+        pivots = [row_of(row[k // 8], k % 8) for k in range(w)] if near else []
+        for t in near:
+            terms = [ahead[t, k] * pivots[k] for k in range(w)]
+            while len(terms) > 1:
+                terms = [functools.reduce(jnp.add, terms[i:i + 2]) for i in range(0, len(terms), 2)]
+            a[t] = jnp.where(inside, 0.0, a[t]) - terms[0]
+        old = jnp.concatenate([a[t] for t in rest], 0)
+        old_h, old_l = two(old)
+        new_h, new_l = two(jnp.concatenate(row, 0))
+        gap = [jnp.zeros((m, n), BF16) for m in (k0, n - k0 - w)]
+
+        def padded(x):
+            return jnp.concatenate([p for p in (gap[0], x, gap[1]) if p.shape[0]], 0)
+
+        high, low = padded(new_h), padded(new_l)
+        change = dot(jnp.concatenate([old_h, old_l], 1), jnp.concatenate([high, high], 0), NN) + dot(old_h, low, NN)
+        for i, t in enumerate(rest):
+            a[t] = jnp.where(inside, 0.0, a[t]) - change[8 * i:8 * i + 8]
         for s in range(wt):
             a[t0 + s] = row[s]
-    for t in range(tiles):
-        store(t, a[t])
+    return jnp.concatenate(a, 0)
 
 
 def write_features(phi_ref, x_ref, u, at):
@@ -169,7 +192,7 @@
 
 def kernel(
     x_ref, u_ref, t_ref, lo_ref, du_ref, co_ref, rh_ref,
-    xo, uo, to, phi, phi_h, phi_l, s_ref, d_ref, p_ref, b_h, b_l, l1_ref,
+    xo, uo, to, phi, phi_h, phi_l, s_ref, d_ref, b_h, b_l, l1_ref,
     outs, ins, mids, zs, zs_far, res, sent, stats,
     pair_sems, send1, recv1, send2, recv2, send3, recv3, send_res, recv_res,
 ):
@@ -222,53 +245,76 @@
     for copy in pair:
         copy.start()
 
-    def eliminate(kb, carry):
-        rows = pl.ds(pl.multiple_of(kb * 128, 128), 128)
-        d_ref[...] = s_ref[rows, rows]
-        invert(lambda t: d_ref[8 * t:8 * t + 8, :], lambda t, v: d_ref.__setitem__((slice(8 * t, 8 * t + 8), slice(None)), v))
-
-        @pl.when(kb == 0)
-        def _():
-            for copy in pair:
-                copy.wait()
-            u_far = uo[...]
-            mine = stacks(x_ref[...], u_ref[...])
-            far = stacks(xo[...], u_far)
-            s_ref[0:MINE, MINE:M] = kernel_block(mine, far)
-            s_ref[MINE:M, 0:MINE] = kernel_block(far, mine)
-            s_ref[MINE:M, MINE:M] = add_diagonal(kernel_block(far, far))
-            write_features(phi, xo, u_far, MINE)
-
-        inverse = d_ref[...]
-        p_ref[...] = dot3(two(inverse), two(s_ref[rows, :]), NN)
-        p_ref[:, rows] = inverse
-        column = two(s_ref[:, rows])
-        s_ref[:, rows] = jnp.zeros((M, 128), F32)
-        row = two(p_ref[...])
+    def block(r, c):
+        return s_ref[128 * r:128 * r + 128, 128 * c:128 * c + 128]
+
+    def next_block(kb, inverse):
+        ahead = dot3(inverse, two(block(kb, kb + 1)), NN)
+        return block(kb + 1, kb + 1) - dot3(two(block(kb + 1, kb)), two(ahead), NN)
+
+    def eliminate(kb, inverse):
+        rows = slice(128 * kb, 128 * kb + 128)
+        high = two(inverse)
+        pivots = jnp.concatenate(
+            [inverse if c == kb else dot3(high, two(block(kb, c)), NN) for c in range(4)], 1
+        )
+        halves = two(pivots)
         for rb in range(4):
-            part = tuple(c[128 * rb:128 * rb + 128] for c in column)
-            s_ref[128 * rb:128 * rb + 128, :] -= dot3(part, row, NN)
-        s_ref[rows, :] = p_ref[...]
-        return carry
-
-    lax.fori_loop(0, 4, eliminate, 0)
-
+            if rb != kb:
+                change = dot3(two(block(rb, kb)), halves, NN)
+                s_ref[128 * rb:128 * rb + 128, rows] = jnp.zeros((128, 128), F32)
+                s_ref[128 * rb:128 * rb + 128, :] -= change
+        s_ref[rows, :] = pivots
+
+    inverse = invert(block(0, 0))
+    pivot = next_block(0, two(inverse))
+    for copy in pair:
+        copy.wait()
+    following = invert(pivot)
+    u_far = uo[...]
+    own = stacks(x_ref[...], u_ref[...])
+    far = stacks(xo[...], u_far)
+    s_ref[0:MINE, MINE:M] = kernel_block(own, far)
+    s_ref[MINE:M, 0:MINE] = kernel_block(far, own)
+    s_ref[MINE:M, MINE:M] = add_diagonal(kernel_block(far, far))
+    eliminate(0, inverse)
+    write_features(phi, xo, u_far, MINE)
+    inverse = following
+
+    pivot = next_block(1, two(inverse))
+    following = invert(pivot)
+    eliminate(1, inverse)
     high, low = two(phi[...])
     phi_h[...] = high
     phi_l[...] = low
-    phis = (phi_h, phi_l)
-
-    def with_phi(a, dims):
-        return dot3(two(a), (phi_h[...], phi_l[...]), dims)
+    inverse = following
+
+    pivot = next_block(2, two(inverse))
+    following = invert(pivot)
+    eliminate(2, inverse)
+    inverse = following
+
+    def phis():
+        return phi_h[...], phi_l[...]
 
     first = feat == 0
     targets = jnp.concatenate(
         [jnp.where(first, t[0:HALF, :], t[HALF:R, :]) for t in (t_ref, to)], 1
     )
-    inverse = two(s_ref[...])
-    w1 = dot3(two(targets), inverse, NN)
-    l1 = with_phi(w1, NT)
+    rest_rows = slice(0, 384)
+    done = s_ref[rest_rows, :]
+    left = rows3(targets[:, rest_rows], two(done), NN)
+    v = targets[:, 384:M] - left[:, 384:M]
+    y = jnp.concatenate([left[:, rest_rows], jnp.zeros((HALF, 128), F32)], 1)
+    ly = rows3(y, phis(), NT)
+    last = two(s_ref[384:M, rest_rows])
+    ph, pl_ = phis()
+    g3 = two(dot3(last, (ph[:, rest_rows], pl_[:, rest_rows]), NT) + phi[:, 384:M].T)
+
+    vd = rows3(v, two(inverse), NN)
+    l1 = ly + rows3(vd, g3, NN)
     l1_ref[...] = l1
+    d_ref[...] = inverse
 
     def remote(src, dst, send, recv, device):
         return pltpu.make_async_remote_copy(
@@ -388,8 +434,10 @@
     lane = lax.broadcasted_iota(jnp.int32, (1, 128), 1)
 
     send_chunks(0, l1)
-    rest = two(w1 - rho * M * dot3(two(w1), inverse, NN))
-    fixed = dot3(rest, (phi_h[...], phi_l[...]), NT)
+    w1 = y + jnp.concatenate([rows3(vd, last, NN), vd], 1)
+    eliminate(3, d_ref[...])
+    inverse = two(s_ref[...])
+    fixed = rows3(w1 - rho * M * rows3(w1, inverse, NN), phis(), NT)
 
     @pl.when(owner)
     def _():
@@ -406,8 +454,7 @@
         stats[...] = jnp.where(lane == 0, primal, jnp.where(lane == 2, dual, 0.0))
 
     z1 = gathered(0)
-    y = two(with_phi(z1, NN))
-    l2 = 2.0 * z1 + (fixed - 2.0 * dot3(y, (b_h[...], b_l[...]), NN))
+    l2 = 2.0 * z1 + (fixed - 2.0 * rows3(rows3(z1, phis(), NN), (b_h[...], b_l[...]), NN))
     u1 = l1_ref[...] - z1
     send_chunks(1, l2 + u1)
     lo_ref[0] = l2[:, 0:FEATS]
@@ -471,7 +518,7 @@
         out_specs=(vmem,) * 4,
         scratch_shapes=[
             f32(R, MINE), f32(1, MINE), f32(R, MINE),
-            f32(WIDE, M), half(WIDE, M), half(WIDE, M), f32(M, M), f32(128, 128), f32(128, M),
+            f32(WIDE, M), half(WIDE, M), half(WIDE, M), f32(M, M), f32(128, 128),
             half(M, WIDE), half(M, WIDE), f32(HALF, WIDE),
             f32(2, PLANE, 9, 128), f32(2, 2 * PLANE, 9, 128), f32(2, DEPTH, 19, 128),
             f32(2, PLANE, 9, 128), f32(2, 9, 128), f32(PLANE, 1, 128), f32(2 * PLANE, 1, 128), f32(1, 128),

time: 61.2 us -> 55 us (0.90)
  Pallas kernels: 55.5 us -> 49.3 us
    pallas_call x1, Pallas kernels: 55.5 us -> 49.3 us  [shards(): pl.pallas_call(kernel, out_shape=(jax.ShapeDtypeStruct((1, HALF, FEATS),...]
where the time goes in v3:
time: 55 us; the launch traced here: 54.7 us
  Pallas kernels  49.3 us (90%)
  local copies, waits for them, and re-layouts  4.84 us (9%)
  between operations  0.65 us (1%)
    pallas_call x1, Pallas kernels, shards(): pl.pallas_call(kernel, out_shape=(jax.ShapeDtypeStruct((1, HALF, FEATS),...  49.3 us
    unnamed x8, local copies, waits for them, and re-layouts  3.43 us
    pallas_call x2, local copies, waits for them, and re-layouts, shards(): pl.pallas_call(kernel, out_shape=(jax.ShapeDtypeStruct((1, HALF, FEATS),...  1.41 us

profile of v3, /device:TPU:1, one launch (start us, length us, event | category | flops | bytes accessed | tf_op | source)
XLA Modules:
  0.0 54.7 jit_solution(7235673139352557420)
XLA Ops:
  0.6 0.0 copy-start.2
  0.6 0.7 %copy-done.2 = f32[256]{0:T(256)S(1)} copy-done((f32[256]{0:T(256)S(1)}, f32[256]{0:T(256)}, u32[]{:S(2)}) %copy-start.2) | copy-done | bytes 1048
  1.3 0.0 copy-start
  1.3 0.8 %copy-done = f32[40,256]{1,0:T(8,128)S(1)} copy-done((f32[40,256]{1,0:T(8,128)S(1)}, f32[40,256]{1,0:T(8,128)}, u32[]{:S(2)}) %copy-start) | copy-done | bytes 40984
  2.1 0.0 copy-start.1
  2.1 0.8 %copy-done.1 = f32[40,256]{1,0:T(8,128)S(1)} copy-done((f32[40,256]{1,0:T(8,128)S(1)}, f32[40,256]{1,0:T(8,128)}, u32[]{:S(2)}) %copy-start.1) | copy-done | bytes 40984
  2.9 49.3 %consensus.1 = (f32[1,20,862]{2,1,0:T(8,128)S(1)}, f32[1,20,862]{2,1,0:T(8,128)S(1)}, f32[20,862]{1,0:T(8,128)S(1)}, f32[2,2]{1,0:T(2,128)S(1)}) custom-call(f32[40,256]{1,0:T(8,128)S(1)} %copy-done, f32[1,256]{1,0:T(1,128)S(1)} %bitcast.1, f32[40,256]{1,0:T(8,128)S(1)} %copy-done.1), custom_call_target="tpu_custom_call" | custom-call | tf_op jit(solution)/shard_map/consensus/pallas_call | solution.py:509
  52.1 0.7 %copy.7 = f32[1,20,862]{2,0,1:T(1,128)} copy(f32[1,20,862]{2,1,0:T(8,128)S(1)} %get-tuple-element.4) | data formatting | bytes 137920 | tf_op jit(solution)/shard_map/consensus/pallas_call | solution.py:509
  52.8 0.7 %copy.8 = f32[1,20,862]{2,0,1:T(1,128)} copy(f32[1,20,862]{2,1,0:T(8,128)S(1)} %get-tuple-element.5) | data formatting | bytes 137920 | tf_op jit(solution)/shard_map/consensus/pallas_call | solution.py:509
  53.5 0.6 %copy.11 = f32[20,862]{1,0:T(8,128)} copy(f32[20,862]{1,0:T(8,128)S(1)} %get-tuple-element.14) | data formatting | bytes 137920
  54.2 0.6 %copy.12 = f32[2,2]{1,0:T(2,128)} copy(f32[2,2]{1,0:T(2,128)S(1)} %get-tuple-element.15) | data formatting | bytes 32
Async XLA Ops:
  0.6 0.7 %copy-start.2 = (f32[256]{0:T(256)S(1)}, f32[256]{0:T(256)}, u32[]{:S(2)}) copy-start(f32[256]{0:T(256)} %param.4) | copy-start | bytes 3076
  1.3 0.8 %copy-start = (f32[40,256]{1,0:T(8,128)S(1)}, f32[40,256]{1,0:T(8,128)}, u32[]{:S(2)}) copy-start(f32[40,256]{1,0:T(8,128)} %x_ref.1) | copy-start | bytes 122884
  2.1 0.8 %copy-start.1 = (f32[40,256]{1,0:T(8,128)S(1)}, f32[40,256]{1,0:T(8,128)}, u32[]{:S(2)}) copy-start(f32[40,256]{1,0:T(8,128)} %t_ref.1) | copy-start | bytes 122884

commit v4 on v3

--- a/solution.py
+++ b/solution.py
@@ -457,7 +457,7 @@
     l2 = 2.0 * z1 + (fixed - 2.0 * rows3(rows3(z1, phis(), NN), (b_h[...], b_l[...]), NN))
     u1 = l1_ref[...] - z1
     send_chunks(1, l2 + u1)
-    lo_ref[0] = l2[:, 0:FEATS]
+    lo_ref[:, 0, :] = l2[:, 0:FEATS]
     l1_ref[...] = u1 + l2
 
     @pl.when(owner)
@@ -472,7 +472,7 @@
         remote(res.at[plane], res.at[plane], send_res.at[0], recv_res.at[0], (slab, 0)).start()
 
     z2 = gathered(1)
-    du_ref[0] = (l1_ref[...] - z2)[:, 0:FEATS]
+    du_ref[:, 0, :] = (l1_ref[...] - z2)[:, 0:FEATS]
     co_ref[...] = z2[:, 0:FEATS]
 
     @pl.when(owner)
@@ -501,19 +501,30 @@
             take(outs.at[k], send1.at[k])
 
 
+def put_out(*refs):
+    sems = refs[-1]
+    copies = [pltpu.make_async_copy(refs[i], refs[4 + i], sems.at[i]) for i in range(4)]
+    for copy in copies:
+        copy.start()
+    for copy in copies:
+        copy.wait()
+
+
 def shards(states, inputs, targets):
     vmem = pl.BlockSpec(memory_space=pltpu.VMEM)
     dma = pltpu.SemaphoreType.DMA
     f32 = lambda *shape: pltpu.VMEM(shape, F32)
     half = lambda *shape: pltpu.VMEM(shape, BF16)
-    return pl.pallas_call(
+    results = (
+        jax.ShapeDtypeStruct((HALF, 1, FEATS), F32),
+        jax.ShapeDtypeStruct((HALF, 1, FEATS), F32),
+        jax.ShapeDtypeStruct((HALF, FEATS), F32),
+        jax.ShapeDtypeStruct((2, 2), F32),
+    )
+    whole = pl.BlockSpec(memory_space=pl.ANY)
+    operators, duals, consensus, history = pl.pallas_call(
         kernel,
-        out_shape=(
-            jax.ShapeDtypeStruct((1, HALF, FEATS), F32),
-            jax.ShapeDtypeStruct((1, HALF, FEATS), F32),
-            jax.ShapeDtypeStruct((HALF, FEATS), F32),
-            jax.ShapeDtypeStruct((2, 2), F32),
-        ),
+        out_shape=results,
         in_specs=[vmem] * 3,
         out_specs=(vmem,) * 4,
         scratch_shapes=[
@@ -529,6 +540,16 @@
         ),
         name="consensus",
     )(states, inputs.reshape(1, MINE), targets)
+    operators, duals, consensus, history = pl.pallas_call(
+        put_out,
+        out_shape=results,
+        in_specs=[vmem] * 4,
+        out_specs=(whole,) * 4,
+        scratch_shapes=[dma((4,))],
+        compiler_params=pltpu.CompilerParams(vmem_limit_bytes=1024 * 1024),
+        name="put_out",
+    )(operators, duals, consensus, history)
+    return operators.transpose(1, 0, 2), duals.transpose(1, 0, 2), consensus, history
 
 
 def solution(mesh):

time: 55 us -> 53.2 us (0.967)
  local copies, waits for them, and re-layouts: 4.84 us -> 2.23 us
  Pallas kernels: 49.3 us -> 50 us
    pallas_call x2 -> x0, local copies, waits for them, and re-layouts: 1.41 us -> none  [shards(): pl.pallas_call(kernel, out_shape=(jax.ShapeDtypeStruct((1, HALF, FEATS),...]
    unnamed x8 -> x6, local copies, waits for them, and re-layouts: 3.43 us -> 2.23 us
    pallas_call x1 -> x2, Pallas kernels: 49.3 us -> 50 us  [the longest x1 49.3 us: shards(): pl.pallas_call(kernel, out_shape=results, in_specs=[vmem] * 3, out_specs=...]
where the time goes in v4:
time: 53.2 us; the launch traced here: 53 us
  Pallas kernels  50 us (94%)
  local copies, waits for them, and re-layouts  2.23 us (4%)
  between operations  0.81 us (2%)
    pallas_call x1, Pallas kernels, shards(): pl.pallas_call(kernel, out_shape=results, in_specs=[vmem] * 3, out_specs=...  49.3 us
    unnamed x6, local copies, waits for them, and re-layouts  2.23 us

profile of v4, /device:TPU:1, one launch (start us, length us, event | category | flops | bytes accessed | tf_op | source)
XLA Modules:
  0.0 53.0 jit_solution(11742795651095480141)
XLA Ops:
  0.6 0.0 copy-start.2
  0.6 0.7 %copy-done.2 = f32[256]{0:T(256)S(1)} copy-done((f32[256]{0:T(256)S(1)}, f32[256]{0:T(256)}, u32[]{:S(2)}) %copy-start.2) | copy-done | bytes 1048
  1.3 0.0 copy-start
  1.3 0.8 %copy-done = f32[40,256]{1,0:T(8,128)S(1)} copy-done((f32[40,256]{1,0:T(8,128)S(1)}, f32[40,256]{1,0:T(8,128)}, u32[]{:S(2)}) %copy-start) | copy-done | bytes 40984
  2.1 0.0 copy-start.1
  2.1 0.8 %copy-done.1 = f32[40,256]{1,0:T(8,128)S(1)} copy-done((f32[40,256]{1,0:T(8,128)S(1)}, f32[40,256]{1,0:T(8,128)}, u32[]{:S(2)}) %copy-start.1) | copy-done | bytes 40984
  2.9 49.3 %consensus.1 = (f32[20,1,862]{2,1,0:T(1,128)S(1)}, f32[20,1,862]{2,1,0:T(1,128)S(1)}, f32[20,862]{1,0:T(8,128)S(1)}, f32[2,2]{1,0:T(2,128)S(1)}) custom-call(f32[40,256]{1,0:T(8,128)S(1)} %copy-done, f32[1,256]{1,0:T(1,128)S(1)} %bitcast.3, f32[40,256]{1,0:T(8,128)S(1)} %copy-done.1), custom_call_target="tpu_custom_call" | custom-call | tf_op jit(solution)/shard_map/consensus/pallas_call | solution.py:525
  52.1 0.7 %put_out.1 = (f32[20,1,862]{2,1,0:T(1,128)}, f32[20,1,862]{2,1,0:T(1,128)}, f32[20,862]{1,0:T(8,128)}, f32[2,2]{1,0:T(2,128)}) custom-call(f32[20,1,862]{2,1,0:T(1,128)S(1)} %get-tuple-element.12.refs_0_, f32[20,1,862]{2,1,0:T(1,128)S(1)} %get-tuple-element.13.refs_1_, f32[20,862]{1,0:T(8,128)S(1)} %get-tuple-element.14.refs_2_, ...), custom_call_target="tpu_custom_call" | custom-call | tf_op jit(solution)/shard_map/put_out/pallas_call | solution.py:543
Async XLA Ops:
  0.6 0.7 %copy-start.2 = (f32[256]{0:T(256)S(1)}, f32[256]{0:T(256)}, u32[]{:S(2)}) copy-start(f32[256]{0:T(256)} %param.4) | copy-start | bytes 3076
  1.3 0.8 %copy-start = (f32[40,256]{1,0:T(8,128)S(1)}, f32[40,256]{1,0:T(8,128)}, u32[]{:S(2)}) copy-start(f32[40,256]{1,0:T(8,128)} %x_ref.1) | copy-start | bytes 122884
  2.1 0.8 %copy-start.1 = (f32[40,256]{1,0:T(8,128)S(1)}, f32[40,256]{1,0:T(8,128)}, u32[]{:S(2)}) copy-start(f32[40,256]{1,0:T(8,128)} %t_ref.1) | copy-start | bytes 122884

commit v5 on v4

--- a/solution.py
+++ b/solution.py
@@ -87,7 +87,8 @@
     return block + jnp.where(row == col, rho * M, 0.0)
 
 
-def invert(a, n=128, w=16):
+def invert(a, beside=(), n=128, w=16):
+    beside = list(beside)
     tiles, wt = n // 8, w // 8
     lane = lax.broadcasted_iota(jnp.int32, (8, n), 1)
     sub = lax.broadcasted_iota(jnp.int32, (8, n), 0)
@@ -110,6 +111,8 @@
         row = [jnp.where(inside, (lane == k0 + 8 * s + sub).astype(F32), a[t0 + s]) for s in range(wt)]
         scale = [None] * wt
         for k in range(w):
+            if k == 4 and beside:
+                beside.pop(0)()
             s0, i = divmod(k, 8)
             inv = 1.0 / row_of(col[k][s0], i)
             scale[s0] = inv if i == 0 else jnp.where(sub == i, inv, scale[s0])
@@ -145,6 +148,8 @@
             a[t] = jnp.where(inside, 0.0, a[t]) - change[8 * i:8 * i + 8]
         for s in range(wt):
             a[t0 + s] = row[s]
+    for work in beside:
+        work()
     return jnp.concatenate(a, 0)
 
 
@@ -191,11 +196,14 @@
 
 
 def kernel(
-    x_ref, u_ref, t_ref, lo_ref, du_ref, co_ref, rh_ref,
-    xo, uo, to, phi, phi_h, phi_l, s_ref, d_ref, b_h, b_l, l1_ref,
+    near_ref, lo_ref, du_ref, co_ref, rh_ref,
+    far_ref, phi, phi_h, phi_l, s_ref, d_ref, p_ref, b_h, b_l, l1_ref,
     outs, ins, mids, zs, zs_far, res, sent, stats,
     pair_sems, send1, recv1, send2, recv2, send3, recv3, send_res, recv_res,
 ):
+    (x_ref, t_ref, u_ref), (xo, to, uo) = (
+        [ref.at[0:R], ref.at[R:2 * R], ref.at[2 * R:2 * R + 1]] for ref in (near_ref, far_ref)
+    )
     slab = lax.axis_index("slab")
     feat = lax.axis_index("feat")
     plane = lax.rem(slab, PLANE)
@@ -235,15 +243,11 @@
     write_features(phi, x_ref, u_own, 0)
 
     pl.semaphore_wait(barrier, PLANE + feat * (PLANE + DEPTH - 2))
-    pair = [
-        pltpu.make_async_remote_copy(
-            src_ref=src, dst_ref=dst, send_sem=pair_sems.at[i], recv_sem=pair_sems.at[3 + i],
-            device_id=(slab, other), device_id_type=MESH,
-        )
-        for i, (src, dst) in enumerate(((x_ref, xo), (u_ref, uo), (t_ref, to)))
-    ]
-    for copy in pair:
-        copy.start()
+    pair = pltpu.make_async_remote_copy(
+        src_ref=near_ref, dst_ref=far_ref, send_sem=pair_sems.at[0], recv_sem=pair_sems.at[1],
+        device_id=(slab, other), device_id_type=MESH,
+    )
+    pair.start()
 
     def block(r, c):
         return s_ref[128 * r:128 * r + 128, 128 * c:128 * c + 128]
@@ -254,63 +258,70 @@
 
     def eliminate(kb, inverse):
         rows = slice(128 * kb, 128 * kb + 128)
-        high = two(inverse)
-        pivots = jnp.concatenate(
-            [inverse if c == kb else dot3(high, two(block(kb, c)), NN) for c in range(4)], 1
-        )
-        halves = two(pivots)
-        for rb in range(4):
-            if rb != kb:
-                change = dot3(two(block(rb, kb)), halves, NN)
-                s_ref[128 * rb:128 * rb + 128, rows] = jnp.zeros((128, 128), F32)
-                s_ref[128 * rb:128 * rb + 128, :] -= change
-        s_ref[rows, :] = pivots
+
+        def pivots():
+            high = two(inverse)
+            p_ref[kb % 2] = jnp.concatenate(
+                [inverse if c == kb else dot3(high, two(block(kb, c)), NN) for c in range(4)], 1
+            )
+
+        def update(rb):
+            change = dot3(two(block(rb, kb)), two(p_ref[kb % 2]), NN)
+            s_ref[128 * rb:128 * rb + 128, rows] = jnp.zeros((128, 128), F32)
+            s_ref[128 * rb:128 * rb + 128, :] -= change
+
+        def close():
+            s_ref[rows, :] = p_ref[kb % 2]
+
+        order = [(kb + i) % 4 for i in range(1, 4)]
+        return [pivots] + [functools.partial(update, rb) for rb in order] + [close]
+
+    def far_blocks():
+        u_far = uo[...]
+        own = stacks(x_ref[...], u_ref[...])
+        far = stacks(xo[...], u_far)
+        s_ref[0:MINE, MINE:M] = kernel_block(own, far)
+        s_ref[MINE:M, 0:MINE] = kernel_block(far, own)
+        s_ref[MINE:M, MINE:M] = add_diagonal(kernel_block(far, far))
+
+    def split_features(i):
+        part = slice(224 * i, 224 * i + 224)
+        phi_h[part], phi_l[part] = two(phi[part])
 
     inverse = invert(block(0, 0))
     pivot = next_block(0, two(inverse))
-    for copy in pair:
-        copy.wait()
-    following = invert(pivot)
-    u_far = uo[...]
-    own = stacks(x_ref[...], u_ref[...])
-    far = stacks(xo[...], u_far)
-    s_ref[0:MINE, MINE:M] = kernel_block(own, far)
-    s_ref[MINE:M, 0:MINE] = kernel_block(far, own)
-    s_ref[MINE:M, MINE:M] = add_diagonal(kernel_block(far, far))
-    eliminate(0, inverse)
-    write_features(phi, xo, u_far, MINE)
-    inverse = following
-
+    pair.wait()
+    inverse = invert(pivot, [far_blocks] + eliminate(0, inverse) + [lambda: write_features(phi, xo, uo[...], MINE)])
     pivot = next_block(1, two(inverse))
-    following = invert(pivot)
-    eliminate(1, inverse)
-    high, low = two(phi[...])
-    phi_h[...] = high
-    phi_l[...] = low
-    inverse = following
-
+    inverse = invert(pivot, eliminate(1, inverse) + [functools.partial(split_features, i) for i in range(4)])
     pivot = next_block(2, two(inverse))
-    following = invert(pivot)
-    eliminate(2, inverse)
-    inverse = following
 
     def phis():
         return phi_h[...], phi_l[...]
 
     first = feat == 0
-    targets = jnp.concatenate(
-        [jnp.where(first, t[0:HALF, :], t[HALF:R, :]) for t in (t_ref, to)], 1
-    )
     rest_rows = slice(0, 384)
-    done = s_ref[rest_rows, :]
-    left = rows3(targets[:, rest_rows], two(done), NN)
-    v = targets[:, 384:M] - left[:, 384:M]
-    y = jnp.concatenate([left[:, rest_rows], jnp.zeros((HALF, 128), F32)], 1)
-    ly = rows3(y, phis(), NT)
-    last = two(s_ref[384:M, rest_rows])
-    ph, pl_ = phis()
-    g3 = two(dot3(last, (ph[:, rest_rows], pl_[:, rest_rows]), NT) + phi[:, 384:M].T)
-
+    kept = {}
+
+    def solve_rest():
+        targets = jnp.concatenate(
+            [jnp.where(first, t[0:HALF, :], t[HALF:R, :]) for t in (t_ref, to)], 1
+        )
+        left = rows3(targets[:, rest_rows], two(s_ref[rest_rows, :]), NN)
+        kept["v"] = targets[:, 384:M] - left[:, 384:M]
+        kept["y"] = jnp.concatenate([left[:, rest_rows], jnp.zeros((HALF, 128), F32)], 1)
+
+    def apply_rest():
+        kept["ly"] = rows3(kept["y"], phis(), NT)
+
+    def last_features():
+        kept["last"] = two(s_ref[384:M, rest_rows])
+        kept["g3"] = two(
+            dot3(kept["last"], (phi_h[:, rest_rows], phi_l[:, rest_rows]), NT) + phi[:, 384:M].T
+        )
+
+    inverse = invert(pivot, eliminate(2, inverse) + [solve_rest, apply_rest, last_features])
+    v, y, ly, last, g3 = (kept[name] for name in ("v", "y", "ly", "last", "g3"))
     vd = rows3(v, two(inverse), NN)
     l1 = ly + rows3(vd, g3, NN)
     l1_ref[...] = l1
@@ -435,7 +446,8 @@
 
     send_chunks(0, l1)
     w1 = y + jnp.concatenate([rows3(vd, last, NN), vd], 1)
-    eliminate(3, d_ref[...])
+    for work in eliminate(3, d_ref[...]):
+        work()
     inverse = two(s_ref[...])
     fixed = rows3(w1 - rho * M * rows3(w1, inverse, NN), phis(), NT)
 
@@ -522,24 +534,25 @@
         jax.ShapeDtypeStruct((2, 2), F32),
     )
     whole = pl.BlockSpec(memory_space=pl.ANY)
+    packed = jnp.concatenate([states, targets, jnp.broadcast_to(inputs[None], (8, MINE))], 0)
     operators, duals, consensus, history = pl.pallas_call(
         kernel,
         out_shape=results,
-        in_specs=[vmem] * 3,
+        in_specs=[vmem],
         out_specs=(vmem,) * 4,
         scratch_shapes=[
-            f32(R, MINE), f32(1, MINE), f32(R, MINE),
-            f32(WIDE, M), half(WIDE, M), half(WIDE, M), f32(M, M), f32(128, 128),
+            f32(2 * R + 8, MINE),
+            f32(WIDE, M), half(WIDE, M), half(WIDE, M), f32(M, M), f32(128, 128), f32(2, 128, M),
             half(M, WIDE), half(M, WIDE), f32(HALF, WIDE),
             f32(2, PLANE, 9, 128), f32(2, 2 * PLANE, 9, 128), f32(2, DEPTH, 19, 128),
             f32(2, PLANE, 9, 128), f32(2, 9, 128), f32(PLANE, 1, 128), f32(2 * PLANE, 1, 128), f32(1, 128),
-            dma((6,)), dma((2,)), dma((2,)), dma((2,)), dma((2,)), dma((2,)), dma((2,)), dma((1,)), dma((1,)),
+            dma((2,)), dma((2,)), dma((2,)), dma((2,)), dma((2,)), dma((2,)), dma((2,)), dma((1,)), dma((1,)),
         ],
         compiler_params=pltpu.CompilerParams(
             collective_id=0, has_side_effects=True, vmem_limit_bytes=48 * 1024 * 1024
         ),
         name="consensus",
-    )(states, inputs.reshape(1, MINE), targets)
+    )(packed)
     operators, duals, consensus, history = pl.pallas_call(
         put_out,
         out_shape=results,

time: 53.2 us -> 50.4 us (0.947)
  Pallas kernels: 50 us -> 48.1 us
  local copies, waits for them, and re-layouts: 2.23 us -> 0.68 us
  other arithmetic: 0 us -> 0.81 us
    unnamed x6 -> x0, local copies, waits for them, and re-layouts: 2.23 us -> none
    pallas_call x1, Pallas kernels: 49.3 us -> 47.4 us  [shards(): pl.pallas_call(kernel, out_shape=results, in_specs=[vmem], out_specs=(vme...]
    concatenate x0 -> x1, other arithmetic: none -> 0.81 us  [shards(): jnp.concatenate([states, targets, jnp.broadcast_to(inputs[None], (8, MINE...]
    broadcast_in_dim x0 -> x1, local copies, waits for them, and re-layouts: none -> 0.68 us  [shards(): jnp.broadcast_to(inputs[None], (8, MINE))]
where the time goes in v5:
time: 50.4 us; the launch traced here: 50.3 us
  Pallas kernels  48.1 us (95%)
  other arithmetic  0.81 us (2%)
  local copies, waits for them, and re-layouts  0.68 us (1%)
  between operations  0.64 us (1%)
    pallas_call x1, Pallas kernels, shards(): pl.pallas_call(kernel, out_shape=results, in_specs=[vmem], out_specs=(vme...  47.4 us

profile of v5, /device:TPU:1, one launch (start us, length us, event | category | flops | bytes accessed | tf_op | source)
XLA Modules:
  0.0 50.3 jit_solution(12754853144414860679)
XLA Ops:
  0.6 0.7 %broadcast_in_dim.2 = f32[8,256]{1,0:T(8,128)S(1)} broadcast(f32[256]{0:T(256)} %param.4), dimensions={1} | broadcast | bytes 9216 | tf_op jit(solution)/shard_map/broadcast_in_dim | solution.py:537
  1.3 0.8 %pad_maximum_fusion.near_ref = f32[88,256]{1,0:T(8,128)S(1)} fusion(f32[8,256]{1,0:T(8,128)S(1)} %broadcast_in_dim.2, f32[40,256]{1,0:T(8,128)} %param.5, f32[40,256]{1,0:T(8,128)} %param.3), kind=kLoop, calls=%fused_computation | loop fusion | flops 45056 | bytes 180224 | tf_op jit(solution)/shard_map/concatenate | solution.py:537
  2.1 47.4 %consensus.1 = (f32[20,1,862]{2,1,0:T(1,128)S(1)}, f32[20,1,862]{2,1,0:T(1,128)S(1)}, f32[20,862]{1,0:T(8,128)S(1)}, f32[2,2]{1,0:T(2,128)S(1)}) custom-call(f32[88,256]{1,0:T(8,128)S(1)} %pad_maximum_fusion.near_ref), custom_call_target="tpu_custom_call" | custom-call | tf_op jit(solution)/shard_map/consensus/pallas_call | solution.py:538
  49.5 0.7 %put_out.1 = (f32[20,1,862]{2,1,0:T(1,128)}, f32[20,1,862]{2,1,0:T(1,128)}, f32[20,862]{1,0:T(8,128)}, f32[2,2]{1,0:T(2,128)}) custom-call(f32[20,1,862]{2,1,0:T(1,128)S(1)} %get-tuple-element.12.refs_0_, f32[20,1,862]{2,1,0:T(1,128)S(1)} %get-tuple-element.13.refs_1_, f32[20,862]{1,0:T(8,128)S(1)} %get-tuple-element.14.refs_2_, ...), custom_call_target="tpu_custom_call" | custom-call | tf_op jit(solution)/shard_map/put_out/pallas_call | solution.py:556

commit v6 on v5

--- a/solution.py
+++ b/solution.py
@@ -37,6 +37,16 @@
 def dot3(a, b, dims):
     (ah, al), (bh, bl) = a, b
     return dot(ah, bh, dims) + (dot(ah, bl, dims) + dot(al, bh, dims))
+
+
+def left3(a):
+    high, low = two(a)
+    return jnp.concatenate([high, low, high], 1)
+
+
+def right3(b):
+    high, low = two(b)
+    return jnp.concatenate([high, high, low], 0)
 
 
 def rows3(a, b, dims):
@@ -143,7 +153,7 @@
             return jnp.concatenate([p for p in (gap[0], x, gap[1]) if p.shape[0]], 0)
 
         high, low = padded(new_h), padded(new_l)
-        change = dot(jnp.concatenate([old_h, old_l], 1), jnp.concatenate([high, high], 0), NN) + dot(old_h, low, NN)
+        change = dot(jnp.concatenate([old_h, old_l, old_h], 1), jnp.concatenate([high, high, low], 0), NN)
         for i, t in enumerate(rest):
             a[t] = jnp.where(inside, 0.0, a[t]) - change[8 * i:8 * i + 8]
         for s in range(wt):
@@ -196,14 +206,12 @@
 
 
 def kernel(
-    near_ref, lo_ref, du_ref, co_ref, rh_ref,
-    far_ref, phi, phi_h, phi_l, s_ref, d_ref, p_ref, b_h, b_l, l1_ref,
-    outs, ins, mids, zs, zs_far, res, sent, stats,
-    pair_sems, send1, recv1, send2, recv2, send3, recv3, send_res, recv_res,
+    near_ref, u_ref, lo_ref, du_ref, co_ref, rh_ref,
+    far_ref, uo, phi, phi_h, phi_l, s_ref, d_ref, p_ref, b_h, b_l, l1_ref,
+    outs, ins, mids, sqs, zs, zs_far, res, sent, stats,
+    pair_sems, send1, recv1, send2, recv2, send3, recv3, send_sq, recv_sq, send_res, recv_res,
 ):
-    (x_ref, t_ref, u_ref), (xo, to, uo) = (
-        [ref.at[0:R], ref.at[R:2 * R], ref.at[2 * R:2 * R + 1]] for ref in (near_ref, far_ref)
-    )
+    (x_ref, t_ref), (xo, to) = ([ref.at[0:R], ref.at[R:2 * R]] for ref in (near_ref, far_ref))
     slab = lax.axis_index("slab")
     feat = lax.axis_index("feat")
     plane = lax.rem(slab, PLANE)
@@ -240,41 +248,44 @@
     u_own = u_ref[...]
     own = stacks(x_ref[...], u_own)
     s_ref[0:MINE, 0:MINE] = add_diagonal(kernel_block(own, own))
-    write_features(phi, x_ref, u_own, 0)
 
     pl.semaphore_wait(barrier, PLANE + feat * (PLANE + DEPTH - 2))
-    pair = pltpu.make_async_remote_copy(
-        src_ref=near_ref, dst_ref=far_ref, send_sem=pair_sems.at[0], recv_sem=pair_sems.at[1],
-        device_id=(slab, other), device_id_type=MESH,
-    )
-    pair.start()
+    pair = [
+        pltpu.make_async_remote_copy(
+            src_ref=src, dst_ref=dst, send_sem=pair_sems.at[i], recv_sem=pair_sems.at[2 + i],
+            device_id=(slab, other), device_id_type=MESH,
+        )
+        for i, (src, dst) in enumerate(((near_ref, far_ref), (u_ref, uo)))
+    ]
+    for copy in pair:
+        copy.start()
 
     def block(r, c):
         return s_ref[128 * r:128 * r + 128, 128 * c:128 * c + 128]
 
     def next_block(kb, inverse):
-        ahead = dot3(inverse, two(block(kb, kb + 1)), NN)
-        return block(kb + 1, kb + 1) - dot3(two(block(kb + 1, kb)), two(ahead), NN)
+        ahead = dot(left3(inverse), right3(block(kb, kb + 1)), NN)
+        return block(kb + 1, kb + 1) - dot(left3(block(kb + 1, kb)), right3(ahead), NN)
 
     def eliminate(kb, inverse):
         rows = slice(128 * kb, 128 * kb + 128)
 
         def pivots():
-            high = two(inverse)
-            p_ref[kb % 2] = jnp.concatenate(
-                [inverse if c == kb else dot3(high, two(block(kb, c)), NN) for c in range(4)], 1
+            left = left3(inverse)
+            new = jnp.concatenate(
+                [inverse if c == kb else dot(left, right3(block(kb, c)), NN) for c in range(4)], 1
             )
+            s_ref[rows, :] = new
+            p_ref[kb % 2] = right3(new)
 
         def update(rb):
-            change = dot3(two(block(rb, kb)), two(p_ref[kb % 2]), NN)
-            s_ref[128 * rb:128 * rb + 128, rows] = jnp.zeros((128, 128), F32)
-            s_ref[128 * rb:128 * rb + 128, :] -= change
-
-        def close():
-            s_ref[rows, :] = p_ref[kb % 2]
-
-        order = [(kb + i) % 4 for i in range(1, 4)]
-        return [pivots] + [functools.partial(update, rb) for rb in order] + [close]
+            at = slice(128 * rb, 128 * rb + 128)
+            change = dot(left3(block(rb, kb)), p_ref[kb % 2], NN)
+            for c in range(4):
+                old = 0.0 if c == kb else block(rb, c)
+                s_ref[at, 128 * c:128 * c + 128] = old - change[:, 128 * c:128 * c + 128]
+
+        return [pivots] + [functools.partial(update, (kb + i) % 4) for i in range(1, 4)]
 
     def far_blocks():
         u_far = uo[...]
@@ -288,13 +299,14 @@
         part = slice(224 * i, 224 * i + 224)
         phi_h[part], phi_l[part] = two(phi[part])
 
-    inverse = invert(block(0, 0))
-    pivot = next_block(0, two(inverse))
-    pair.wait()
+    inverse = invert(block(0, 0), [lambda: write_features(phi, x_ref, u_ref[...], 0)])
+    pivot = next_block(0, inverse)
+    for copy in pair:
+        copy.wait()
     inverse = invert(pivot, [far_blocks] + eliminate(0, inverse) + [lambda: write_features(phi, xo, uo[...], MINE)])
-    pivot = next_block(1, two(inverse))
+    pivot = next_block(1, inverse)
     inverse = invert(pivot, eliminate(1, inverse) + [functools.partial(split_features, i) for i in range(4)])
-    pivot = next_block(2, two(inverse))
+    pivot = next_block(2, inverse)
 
     def phis():
         return phi_h[...], phi_l[...]
@@ -376,23 +388,28 @@
 
     def average(k):
         take(ins.at[k, 0:2 * PLANE - 1], recv1.at[k])
+        totals = [add_up([parts(ins, k, PLANE * half + s) for s in range(PLANE)]) for half in range(2)]
+        for half in range(2):
+            mids[k, depth, 8 * half:8 * half + 8, :] = totals[half][0]
+            mids[k, depth, 16 + half:17 + half, :] = totals[half][1]
+        for peer in far_depths:
+            remote(
+                mids.at[k, depth], mids.at[k, depth], send2.at[k], recv2.at[k], (in_depth(peer), 1)
+            ).start()
         spread = jnp.zeros((1, 128), F32)
         for half in range(2):
-            sent = [parts(ins, k, PLANE * half + s) for s in range(PLANE)]
-            total = mean = add_up(sent)
-            operators = sent
+            mean = totals[half]
+            operators = [parts(ins, k, PLANE * half + s) for s in range(PLANE)]
             if k == 1:
                 last = consensus_of(0, half)
                 before = [parts(ins, 0, PLANE * half + s) for s in range(PLANE)]
-                operators = [[p - (b - z) for p, b, z in zip(new, old, last)] for new, old in zip(sent, before)]
+                operators = [[p - (b - z) for p, b, z in zip(new, old, last)] for new, old in zip(operators, before)]
                 mean = add_up(operators)
-            mids[k, depth, 8 * half:8 * half + 8, :] = total[0]
-            mids[k, depth, 16 + half:17 + half, :] = total[1]
             spread = spread + squares(operators, [m / PLANE for m in mean])
-        mids[k, depth, 18:19, :] = spread
+        sqs[k, depth] = spread
         for peer in far_depths:
             remote(
-                mids.at[k, depth], mids.at[k, depth], send2.at[k], recv2.at[k], (in_depth(peer), 1)
+                sqs.at[k, depth], sqs.at[k, depth], send_sq.at[k], recv_sq.at[k], (in_depth(peer), 1)
             ).start()
 
     def conclude(k):
@@ -414,6 +431,7 @@
         gather(zs_far.at[k], plane, 0)
 
     def statistics(k):
+        take(sqs.at[k, 0:DEPTH - 1], recv_sq.at[k])
         primal = jnp.zeros((1, 128), F32)
         dual = jnp.zeros((1, 128), F32)
         for half in range(2):
@@ -428,7 +446,7 @@
             primal = primal + PLANE * squares([[p / PLANE for p in each] for each in layers], mean)
             dual = dual + squares([mean], last)
         for z in range(DEPTH):
-            primal = primal + mids[k, z, 18:19, :]
+            primal = primal + sqs[k, z]
         return jnp.sum(primal, 1, keepdims=True), N_SLAB * rho * rho * jnp.sum(dual, 1, keepdims=True)
 
     def gathered(k):
@@ -504,6 +522,7 @@
         for k in range(2):
             take(outs.at[k, 0:PLANE - 1], send1.at[k])
             take(mids.at[k, 0:DEPTH - 1], send2.at[k])
+            take(sqs.at[k, 0:DEPTH - 1], send_sq.at[k])
             take(ins.at[k, 0:2 * PLANE - 1], send3.at[k])
         take(sent.at[0:2 * PLANE - 1], send_res.at[0])
 
@@ -534,25 +553,25 @@
         jax.ShapeDtypeStruct((2, 2), F32),
     )
     whole = pl.BlockSpec(memory_space=pl.ANY)
-    packed = jnp.concatenate([states, targets, jnp.broadcast_to(inputs[None], (8, MINE))], 0)
+    packed = jnp.concatenate([states, targets], 0)
     operators, duals, consensus, history = pl.pallas_call(
         kernel,
         out_shape=results,
-        in_specs=[vmem],
+        in_specs=[vmem] * 2,
         out_specs=(vmem,) * 4,
         scratch_shapes=[
-            f32(2 * R + 8, MINE),
-            f32(WIDE, M), half(WIDE, M), half(WIDE, M), f32(M, M), f32(128, 128), f32(2, 128, M),
+            f32(2 * R, MINE), f32(1, MINE),
+            f32(WIDE, M), half(WIDE, M), half(WIDE, M), f32(M, M), f32(128, 128), half(2, 384, M),
             half(M, WIDE), half(M, WIDE), f32(HALF, WIDE),
-            f32(2, PLANE, 9, 128), f32(2, 2 * PLANE, 9, 128), f32(2, DEPTH, 19, 128),
+            f32(2, PLANE, 9, 128), f32(2, 2 * PLANE, 9, 128), f32(2, DEPTH, 18, 128), f32(2, DEPTH, 1, 128),
             f32(2, PLANE, 9, 128), f32(2, 9, 128), f32(PLANE, 1, 128), f32(2 * PLANE, 1, 128), f32(1, 128),
-            dma((2,)), dma((2,)), dma((2,)), dma((2,)), dma((2,)), dma((2,)), dma((2,)), dma((1,)), dma((1,)),
+            dma((4,)), dma((2,)), dma((2,)), dma((2,)), dma((2,)), dma((2,)), dma((2,)), dma((2,)), dma((2,)), dma((1,)), dma((1,)),
         ],
         compiler_params=pltpu.CompilerParams(
             collective_id=0, has_side_effects=True, vmem_limit_bytes=48 * 1024 * 1024
         ),
         name="consensus",
-    )(packed)
+    )(packed, inputs.reshape(1, MINE))
     operators, duals, consensus, history = pl.pallas_call(
         put_out,
         out_shape=results,

time: 50.4 us -> 49.8 us (0.988)
  local copies, waits for them, and re-layouts: 0.68 us -> 0.01 us
    broadcast_in_dim x1 -> x0, local copies, waits for them, and re-layouts: 0.68 us -> none  [shards(): jnp.broadcast_to(inputs[None], (8, MINE))]
where the time goes in v6:
time: 49.8 us; the launch traced here: 49.7 us
  Pallas kernels  48.2 us (97%)
  other arithmetic  0.81 us (2%)
  between operations  0.65 us (1%)
    pallas_call x1, Pallas kernels, shards(): pl.pallas_call(kernel, out_shape=results, in_specs=[vmem] * 2, out_specs=...  47.5 us

profile of v6, /device:TPU:1, one launch (start us, length us, event | category | flops | bytes accessed | tf_op | source)
XLA Modules:
  0.0 49.7 jit_solution(5853526294893078026)
XLA Ops:
  0.6 0.0 copy-start
  0.6 0.8 %pad_maximum_fusion.near_ref = f32[80,256]{1,0:T(8,128)S(1)} fusion(f32[40,256]{1,0:T(8,128)} %param.5, f32[40,256]{1,0:T(8,128)} %param.3), kind=kLoop, calls=%fused_computation | loop fusion | flops 20480 | bytes 163840 | tf_op jit(solution)/shard_map/concatenate | solution.py:556
  1.5 0.0 copy-done
  1.5 47.5 %consensus.1 = (f32[20,1,862]{2,1,0:T(1,128)S(1)}, f32[20,1,862]{2,1,0:T(1,128)S(1)}, f32[20,862]{1,0:T(8,128)S(1)}, f32[2,2]{1,0:T(2,128)S(1)}) custom-call(f32[80,256]{1,0:T(8,128)S(1)} %pad_maximum_fusion.near_ref, f32[1,256]{1,0:T(1,128)S(1)} %bitcast.3), custom_call_target="tpu_custom_call" | custom-call | tf_op jit(solution)/shard_map/consensus/pallas_call | solution.py:557
  49.0 0.7 %put_out.1 = (f32[20,1,862]{2,1,0:T(1,128)}, f32[20,1,862]{2,1,0:T(1,128)}, f32[20,862]{1,0:T(8,128)}, f32[2,2]{1,0:T(2,128)}) custom-call(f32[20,1,862]{2,1,0:T(1,128)S(1)} %get-tuple-element.12.refs_0_, f32[20,1,862]{2,1,0:T(1,128)S(1)} %get-tuple-element.13.refs_1_, f32[20,862]{1,0:T(8,128)S(1)} %get-tuple-element.14.refs_2_, ...), custom_call_target="tpu_custom_call" | custom-call | tf_op jit(solution)/shard_map/put_out/pallas_call | solution.py:575
Async XLA Ops:
  0.6 0.8 %copy-start = (f32[256]{0:T(256)S(1)}, f32[256]{0:T(256)}, u32[]{:S(2)}) copy-start(f32[256]{0:T(256)} %param.4) | copy-start | bytes 3076

commit v7 on v6

--- a/solution.py
+++ b/solution.py
@@ -249,7 +249,6 @@
     own = stacks(x_ref[...], u_own)
     s_ref[0:MINE, 0:MINE] = add_diagonal(kernel_block(own, own))
 
-    pl.semaphore_wait(barrier, PLANE + feat * (PLANE + DEPTH - 2))
     pair = [
         pltpu.make_async_remote_copy(
             src_ref=src, dst_ref=dst, send_sem=pair_sems.at[i], recv_sem=pair_sems.at[2 + i],
@@ -257,8 +256,10 @@
         )
         for i, (src, dst) in enumerate(((near_ref, far_ref), (u_ref, uo)))
     ]
-    for copy in pair:
-        copy.start()
+    def meet():
+        pl.semaphore_wait(barrier, PLANE + feat * (PLANE + DEPTH - 2))
+        for copy in pair:
+            copy.start()
 
     def block(r, c):
         return s_ref[128 * r:128 * r + 128, 128 * c:128 * c + 128]
@@ -299,7 +300,7 @@
         part = slice(224 * i, 224 * i + 224)
         phi_h[part], phi_l[part] = two(phi[part])
 
-    inverse = invert(block(0, 0), [lambda: write_features(phi, x_ref, u_ref[...], 0)])
+    inverse = invert(block(0, 0), [meet, lambda: write_features(phi, x_ref, u_ref[...], 0)])
     pivot = next_block(0, inverse)
     for copy in pair:
         copy.wait()

time: 49.8 us -> 50.3 us (1.010)
  no operation moved by 1% of the time
where the time goes in v7:
time: 50.3 us; the launch traced here: 50.1 us
  Pallas kernels  48.7 us (97%)
  other arithmetic  0.81 us (2%)
  between operations  0.65 us (1%)
    pallas_call x1, Pallas kernels, shards(): pl.pallas_call(kernel, out_shape=results, in_specs=[vmem] * 2, out_specs=...  47.9 us

profile of v7, /device:TPU:1, one launch (start us, length us, event | category | flops | bytes accessed | tf_op | source)
XLA Modules:
  0.0 50.1 jit_solution(7838578211494200176)
XLA Ops:
  0.6 0.0 copy-start
  0.6 0.8 %pad_maximum_fusion.near_ref = f32[80,256]{1,0:T(8,128)S(1)} fusion(f32[40,256]{1,0:T(8,128)} %param.5, f32[40,256]{1,0:T(8,128)} %param.3), kind=kLoop, calls=%fused_computation | loop fusion | flops 20480 | bytes 163840 | tf_op jit(solution)/shard_map/concatenate | solution.py:557
  1.5 0.0 copy-done
  1.5 47.9 %consensus.1 = (f32[20,1,862]{2,1,0:T(1,128)S(1)}, f32[20,1,862]{2,1,0:T(1,128)S(1)}, f32[20,862]{1,0:T(8,128)S(1)}, f32[2,2]{1,0:T(2,128)S(1)}) custom-call(f32[80,256]{1,0:T(8,128)S(1)} %pad_maximum_fusion.near_ref, f32[1,256]{1,0:T(1,128)S(1)} %bitcast.3), custom_call_target="tpu_custom_call" | custom-call | tf_op jit(solution)/shard_map/consensus/pallas_call | solution.py:558
  49.4 0.7 %put_out.1 = (f32[20,1,862]{2,1,0:T(1,128)}, f32[20,1,862]{2,1,0:T(1,128)}, f32[20,862]{1,0:T(8,128)}, f32[2,2]{1,0:T(2,128)}) custom-call(f32[20,1,862]{2,1,0:T(1,128)S(1)} %get-tuple-element.12.refs_0_, f32[20,1,862]{2,1,0:T(1,128)S(1)} %get-tuple-element.13.refs_1_, f32[20,862]{1,0:T(8,128)S(1)} %get-tuple-element.14.refs_2_, ...), custom_call_target="tpu_custom_call" | custom-call | tf_op jit(solution)/shard_map/put_out/pallas_call | solution.py:576
Async XLA Ops:
  0.6 0.8 %copy-start = (f32[256]{0:T(256)S(1)}, f32[256]{0:T(256)}, u32[]{:S(2)}) copy-start(f32[256]{0:T(256)} %param.4) | copy-start | bytes 3076
